TPU v7x, 32 devices: a whole 2x2x4 slice. The times are simulated.
32 devices in a mesh: scene: 4 (over y, core), tile: 8 (over z, x).
Axes of the slice: x: 2, y: 2, z: 4, core: 2. Of those that a mesh axis runs over, the one named last changes fastest.
Arguments:
- node_latent: bfloat16 [131072, 128], P(('scene', 'tile')), parts along dimension 0, may hold values from -6 to 6
- cotangent: float32 [131072, 128], P(('scene', 'tile')), parts along dimension 0, may hold values from -6 to 6
- neighbours: int32 [12, 131072], P(None, ('scene', 'tile')), parts along dimension 1, may hold values from -1 to 6143, as said below
- send_rows: int32 [32, 2, 1024], P(('scene', 'tile')), parts along dimension 0, may hold values from 0 to 4095
- node_mask: int32 [131072], P(('scene', 'tile')), parts along dimension 0, may hold values 0 or 1
- w_src: bfloat16 [128, 128], replicated, may hold values from -0.5 to 0.5
- w_dst: bfloat16 [128, 128], replicated, may hold values from -0.5 to 0.5
- w_msg: bfloat16 [128, 128], replicated, may hold values from -0.5 to 0.5
- edge_gain: float32 [128], replicated, may hold values from 0.1 to 1.9
- edge_bias: float32 [128], replicated, may hold values from -3 to 3
- w_self: bfloat16 [128, 128], replicated, may hold values from -0.5 to 0.5
- w_agg: bfloat16 [128, 128], replicated, may hold values from -0.5 to 0.5
- node_bias: float32 [128], replicated, may hold values from -3 to 3
- w_out: bfloat16 [128, 128], replicated, may hold values from -0.5 to 0.5
Outputs:
- updated: bfloat16 [131072, 128], P(('scene', 'tile')), parts along dimension 0
- latent_grad: float32 [131072, 128], P(('scene', 'tile')), parts along dimension 0
- grad_src: float32 [512, 128], P('scene'), parts along dimension 0
- grad_dst: float32 [512, 128], P('scene'), parts along dimension 0
- grad_msg: float32 [512, 128], P('scene'), parts along dimension 0
- grad_edge_gain: float32 [512], P('scene'), parts along dimension 0
- grad_edge_bias: float32 [512], P('scene'), parts along dimension 0
- grad_self: float32 [512, 128], P('scene'), parts along dimension 0
- grad_agg: float32 [512, 128], P('scene'), parts along dimension 0
- grad_node_bias: float32 [512], P('scene'), parts along dimension 0
- grad_out: float32 [512, 128], P('scene'), parts along dimension 0
There are 4 independent parts, one for each index of `scene`. A program takes and returns all parts, laid end to end along the dimension named above; an argument that names none is the same for every part. Nothing has to cross between parts.
Inputs may be any that keep to these rules, and one draw needn't show every extreme that they name: `neighbours`: each entry is -1 (empty slot) or a row of the tile's extended list: below 4096 its own nodes, then 1024 rows from the tile below, then 1024 rows from the tile above. `send_rows`: rows of the sending tile's own nodes; a row may appear more than once.
All inputs are finite; a program needn't handle non-finite values. No bound on the sum of `node_mask` on one device may be relied on, other than what follows from the above.
Results may differ from a plain program's by a relative error of at most 0.028.
Values may be sent and summed in bfloat16 or wider, within the bound.
A program may use at most 448 MiB of HBM per device.

v0:
```python
import functools

import jax
import jax.numpy as jnp
from jax import lax
from jax.experimental import pallas as pl
from jax.experimental.pallas import tpu as pltpu
from jax.sharding import PartitionSpec as P

BLOCK = 128
COPIES = 12
BF = jnp.bfloat16
F32 = jnp.float32


def mm(a, b):
    return jnp.dot(a, b, preferred_element_type=F32)


def mm_nt(a, b):
    return lax.dot_general(a, b, (((1,), (1,)), ((), ())), preferred_element_type=F32)


def mm_tn(a, b):
    return lax.dot_general(a, b, (((0,), (0,)), ((), ())), preferred_element_type=F32)


def sigmoid(x):
    return 0.5 * jnp.tanh(0.5 * x) + 0.5


def layer_kernel(
    degree,
    idx_ref,
    own_ref,
    ct_ref,
    cols_ref,
    ext_ref,
    w_src_ref,
    w_dst_ref,
    w_msg_ref,
    w_cent_ref,
    gain_ref,
    ebias_ref,
    w_self_ref,
    w_agg_ref,
    nbias_ref,
    w_out_ref,
    updated_ref,
    down_ref,
    dext_ref,
    gw_ref,
    gv_ref,
    table,
    rows,
    hid,
    slope,
    yhat,
    rstd,
    dmsg,
    *accs,
):
    step = pl.program_id(0)
    count = own_ref.shape[0]
    width = own_ref.shape[1]
    copies = len(accs)
    edges = degree * count
    unroll = 4 * copies

    @pl.when(step == 0)
    def _():
        table[...] = mm(ext_ref[...], w_src_ref[...])
        for acc in accs:
            acc[...] = jnp.zeros_like(acc)
        gw_ref[...] = jnp.zeros_like(gw_ref)
        gv_ref[...] = jnp.zeros_like(gv_ref)

    def gather(t, carry):
        base = pl.multiple_of(t * unroll, unroll)
        for j in range(unroll):
            i = idx_ref[0, 0, base + j]
            rows[pl.ds(base + j, 1), :] = table[pl.ds(i, 1), :]
        return carry

    lax.fori_loop(0, edges // unroll, gather, 0)

    own = own_ref[...]
    ones = jnp.full((width, width), 1.0 / width, BF)
    gain = gain_ref[...]
    pd = mm(own, w_dst_ref[...]) + ebias_ref[...]
    cols = cols_ref[...]

    def present(k):
        return jnp.broadcast_to((cols[:, k : k + 1] >= 0).astype(F32), (count, width))

    ysum = jnp.zeros((count, width), F32)
    for k in range(degree):
        at = pl.ds(k * count, count)
        x = rows[at, :] + pd
        s = sigmoid(x)
        h = x * s
        hb = h.astype(BF)
        hid[at, :] = hb
        slope[at, :] = s + h - h * s
        c = mm(hb, w_cent_ref[...])
        var = mm((c * c).astype(BF), ones)
        r = lax.rsqrt(var + 1e-5)
        y = c * r
        m = present(k)
        yhat[at, :] = y
        rstd[at, :] = r * m
        ysum = ysum + y * m

    sb = (ysum * gain).astype(BF)
    pre = mm(own, w_self_ref[...]) + mm(sb, w_agg_ref[...]) + nbias_ref[...]
    s = sigmoid(pre)
    u = pre * s
    ub = u.astype(BF)
    live = jnp.broadcast_to(cols[:, degree : degree + 1], (count, width)).astype(F32)
    ct = ct_ref[...]
    updated_ref[...] = (own.astype(F32) + live * mm(ub, w_out_ref[...])).astype(BF)
    dob = (live * ct).astype(BF)
    dpre = mm_nt(dob, w_out_ref[...]) * (s + u - u * s)
    dpb = dpre.astype(BF)
    dsum = mm_nt(dpb, w_agg_ref[...])
    dy = dsum * gain
    dyc = dy - jnp.mean(dy, axis=1, keepdims=True)

    dpd = jnp.zeros((count, width), F32)
    for k in range(degree):
        at = pl.ds(k * count, count)
        y = yhat[at, :]
        t = mm((dyc * y).astype(BF), ones)
        dm = (rstd[at, :] * (dyc - y * t)).astype(BF)
        dmsg[at, :] = dm
        dx = mm_nt(dm, w_msg_ref[...]) * slope[at, :]
        rows[at, :] = dx
        dpd = dpd + dx

    dpdb = dpd.astype(BF)
    down_ref[...] = ct + mm_nt(dpb, w_self_ref[...]) + mm_nt(dpdb, w_dst_ref[...])
    gw_ref[1] += mm_tn(own, dpdb)
    gw_ref[2] += mm_tn(hid[...], dmsg[...])
    gw_ref[3] += mm_tn(own, dpb)
    gw_ref[4] += mm_tn(sb, dpb)
    gw_ref[5] += mm_tn(ub, dob)
    gv_ref[0:1] += jnp.sum(dsum * ysum, axis=0, keepdims=True)
    gv_ref[1:2] += jnp.sum(dpd, axis=0, keepdims=True)
    gv_ref[2:3] += jnp.sum(dpre, axis=0, keepdims=True)

    def scatter(t, carry):
        base = pl.multiple_of(t * unroll, unroll)
        for first in range(0, unroll, copies):
            where = [idx_ref[0, 0, base + first + j] for j in range(copies)]
            total = [
                accs[j][pl.ds(where[j], 1), :] + rows[pl.ds(base + first + j, 1), :]
                for j in range(copies)
            ]
            for j in range(copies):
                accs[j][pl.ds(where[j], 1), :] = total[j]
        return carry

    lax.fori_loop(0, edges // unroll, scatter, 0)

    @pl.when(step == pl.num_programs(0) - 1)
    def _():
        dproj = accs[0][...]
        for acc in accs[1:]:
            dproj = dproj + acc[...]
        dpb = dproj.astype(BF)
        dext_ref[...] = mm_nt(dpb, w_src_ref[...])
        gw_ref[0] = mm_tn(ext_ref[...], dpb)


def layer(extended, node_latent, cotangent, neighbours, node_mask, weights):
    w_src, w_dst, w_msg, edge_gain, edge_bias, w_self, w_agg, node_bias, w_out = weights
    degree, nodes = neighbours.shape
    width = node_latent.shape[1]
    listed = extended.shape[0]
    count = min(BLOCK, nodes)
    blocks = nodes // count
    idx = jnp.maximum(neighbours, 0).reshape(degree, blocks, count)
    idx = idx.transpose(1, 0, 2).reshape(blocks, 1, degree * count)
    cols = jnp.concatenate([neighbours, node_mask[None]], axis=0).T
    w32 = w_msg.astype(F32)
    w_cent = (w32 - jnp.mean(w32, axis=1, keepdims=True)).astype(BF)
    whole = lambda shape: pl.BlockSpec(shape, lambda i: (0,) * len(shape))
    mat = whole((width, width))
    vec = whole((1, width))
    rowed = pl.BlockSpec((count, width), lambda i: (i, 0))
    edges = degree * count
    return pl.pallas_call(
        functools.partial(layer_kernel, degree),
        grid=(blocks,),
        in_specs=[
            pl.BlockSpec((1, 1, edges), lambda i: (i, 0, 0), memory_space=pltpu.SMEM),
            rowed,
            rowed,
            pl.BlockSpec((count, degree + 1), lambda i: (i, 0)),
            whole((listed, width)),
            mat,
            mat,
            mat,
            mat,
            vec,
            vec,
            mat,
            mat,
            vec,
            mat,
        ],
        out_specs=[
            rowed,
            rowed,
            whole((listed, width)),
            whole((6, width, width)),
            whole((8, width)),
        ],
        out_shape=[
            jax.ShapeDtypeStruct((nodes, width), BF),
            jax.ShapeDtypeStruct((nodes, width), F32),
            jax.ShapeDtypeStruct((listed, width), F32),
            jax.ShapeDtypeStruct((6, width, width), F32),
            jax.ShapeDtypeStruct((8, width), F32),
        ],
        scratch_shapes=[
            pltpu.VMEM((listed, width), F32),
            pltpu.VMEM((edges, width), F32),
            pltpu.VMEM((edges, width), BF),
            pltpu.VMEM((edges, width), F32),
            pltpu.VMEM((edges, width), F32),
            pltpu.VMEM((edges, width), F32),
            pltpu.VMEM((edges, width), BF),
        ]
        + [pltpu.VMEM((listed, width), F32)] * COPIES,
        compiler_params=pltpu.CompilerParams(
            dimension_semantics=("arbitrary",), vmem_limit_bytes=60 * 2**20
        ),
        name="layer",
    )(
        idx,
        node_latent,
        cotangent,
        cols,
        extended,
        w_src,
        w_dst,
        w_msg,
        w_cent,
        edge_gain[None],
        edge_bias[None],
        w_self,
        w_agg,
        node_bias[None],
        w_out,
    )


def finish_kernel(list_ref, back_ref, dext_ref, down_ref, out_ref):
    count = out_ref.shape[0]
    first = pl.program_id(0) * count
    total = dext_ref[...] + down_ref[...]
    span = list_ref.shape[1]
    here = lax.broadcasted_iota(jnp.int32, (count, span), 0) + first
    hit = jnp.where(here == list_ref[...], 1.0, 0.0).astype(BF)
    out_ref[...] = total + mm(hit, back_ref[...])


def finish(listing, back, dext, down):
    nodes, width = down.shape
    count = min(512, nodes)
    rowed = pl.BlockSpec((count, width), lambda i: (i, 0))
    return pl.pallas_call(
        finish_kernel,
        grid=(nodes // count,),
        in_specs=[
            pl.BlockSpec((1, listing.shape[1]), lambda i: (0, 0)),
            pl.BlockSpec(back.shape, lambda i: (0, 0)),
            rowed,
            rowed,
        ],
        out_specs=rowed,
        out_shape=jax.ShapeDtypeStruct((nodes, width), F32),
        compiler_params=pltpu.CompilerParams(
            dimension_semantics=("arbitrary",), vmem_limit_bytes=60 * 2**20
        ),
        name="finish",
    )(listing, back, dext, down)


def total_over(value, axis):
    size = lax.axis_size(axis)
    if size & (size - 1):
        return lax.psum(value, axis)
    bit = 1
    while bit < size:
        other = lax.ppermute(value, axis, [(i, i ^ bit) for i in range(size)])
        value = (value.astype(F32) + other.astype(F32)).astype(BF)
        bit *= 2
    return value


def on_device(node_latent, cotangent, neighbours, send_rows, node_mask, *weights):
    nodes = node_latent.shape[0]
    rim = send_rows.shape[2]
    size = lax.axis_size("tile")
    up = [(i, (i + 1) % size) for i in range(size)]
    down = [(j, i) for i, j in up]
    listing = send_rows.reshape(1, 2 * rim)
    outbound = node_latent[listing[0]]
    before = lax.ppermute(outbound[rim:], "tile", up)
    after = lax.ppermute(outbound[:rim], "tile", down)
    extended = jnp.concatenate([node_latent, before, after], axis=0)
    updated, down_grad, dext, gw, gv = layer(
        extended, node_latent, cotangent, neighbours, node_mask, weights
    )
    halo = dext[nodes:].astype(BF)
    to_below = lax.ppermute(halo[:rim], "tile", down)
    to_above = lax.ppermute(halo[rim:], "tile", up)
    back = jnp.concatenate([to_above, to_below], axis=0)
    packed = jnp.concatenate([gw.reshape(-1, gw.shape[2]), gv], axis=0).astype(BF)
    packed = total_over(packed, "tile").astype(F32)
    latent_grad = finish(listing, back, dext, down_grad)
    packed = packed * (nodes * size) ** (-0.5)
    width = gw.shape[2]
    mats = [packed[i * width : (i + 1) * width] for i in range(6)]
    vecs = [packed[6 * width + i] for i in range(3)]
    return (
        updated,
        latent_grad,
        mats[0],
        mats[1],
        mats[2],
        vecs[0],
        vecs[1],
        mats[3],
        mats[4],
        vecs[2],
        mats[5],
    )


def solution(mesh):
    rowed, shared = P(("scene", "tile"), None), P()
    in_specs = (
        rowed,
        rowed,
        P(None, ("scene", "tile")),
        P(("scene", "tile"), None, None),
        P(("scene", "tile")),
    ) + (shared,) * 9
    mat, vec = P("scene", None), P("scene")
    out_specs = (rowed, rowed, mat, mat, mat, vec, vec, mat, mat, vec, mat)
    return jax.shard_map(
        on_device, mesh=mesh, in_specs=in_specs, out_specs=out_specs, check_vma=False
    )
```

profile of v0, /device:TPU:14, one launch (start us, length us, event | category | flops | bytes accessed | tf_op | source)
XLA Modules:
  0.0 239.4 jit_solution(735164516113555849)
XLA Ops:
  0.6 0.7 copy.35
  1.4 7.0 %gather_fusion = bf16[2048,128]{1,0:T(8,128)(2,1)S(1)} fusion(bf16[4096,128]{1,0:T(8,128)(2,1)} %own_ref.1, s32[2048]{0:T(1024)S(1)} %broadcast_clamp_fusion), kind=kCustom, calls=%fused_computation | custom fusion | bytes 1056768 | tf_op jit(solution)/shard_map/gather | solution.py:310
  8.5 1.6 collective-permute-start
  10.1 0.5 collective-permute-start.1
  11.0 0.9 reshape.79.idx_ref
  11.9 2.0 copy.32
  13.8 0.7 fusion.w_cent_ref
  14.5 7.7 %collective-permute-done = bf16[1024,128]{1,0:T(8,128)(2,1)S(1)} collective-permute-done((bf16[1024,128]{1,0:T(8,128)(2,1)S(1)}, bf16[1024,128]{1,0:T(8,128)(2,1)S(1)}, u32[]{:S(2)}, u32[]{:S(2)}) %collective-permute-start) | collective-permute-done | bytes 262176 | tf_op jit(solution)/shard_map/ppermute | solution.py:311
  22.2 1.3 pad_maximum_fusion.ext_ref
  23.5 177.6 %layer.1 = (bf16[4096,128]{1,0:T(8,128)(2,1)}, f32[4096,128]{1,0:T(8,128)}, f32[6144,128]{1,0:T(8,128)}, f32[6,128,128]{2,1,0:T(8,128)}, f32[8,128]{1,0:T(8,128)}) custom-call(s32[32,1,1536]{2,1,0:T(1,128)} %reshape.79.idx_ref, bf16[4096,128]{1,0:T(8,128)(2,1)} %own_ref.1, f32[4096,128]{1,0:T(8,128)} %ct_ref.1, s32[4096,13]{1,0:T(8,128)} %bitcast.24, ...), custom_call_target="tpu_custom_call" | custom-call | tf_op jit(solution)/shard_map/layer/pallas_call | solution.py:192
  201.2 0.7 convert.12
  201.8 1.0 convert.11
  202.9 1.5 collective-permute-start.4
  204.4 2.0 convert.10
  206.4 3.1 %collective-permute-done.4 = bf16[776,128]{1,0:T(8,128)(2,1)S(1)} collective-permute-done((bf16[776,128]{1,0:T(8,128)(2,1)S(1)}, bf16[776,128]{1,0:T(8,128)(2,1)S(1)}, u32[]{:S(2)}, u32[]{:S(2)}) %collective-permute-start.4) | collective-permute-done | bytes 198688 | tf_op jit(solution)/shard_map/ppermute | solution.py:297
  209.7 4.4 %collective-permute-start.2 = (bf16[1024,128]{1,0:T(8,128)(2,1)S(1)}, bf16[1024,128]{1,0:T(8,128)(2,1)S(1)}, u32[]{:S(2)}, u32[]{:S(2)}) collective-permute-start(bf16[1024,128]{1,0:T(8,128)(2,1)S(1)} %get-tuple-element.21), channel_id=1, source_target_pairs={{0,1},{1,2},{2,3},{3,4},{4,5},{5,6},{6,7},{7,0},{8,9},{9,10},{10,1... | collective-permute-start | bytes 786440 | tf_op jit(solution)/shard_map/ppermute | solution.py:319
  214.0 3.4 %collective-permute-done.5 = bf16[776,128]{1,0:T(8,128)(2,1)S(1)} collective-permute-done((bf16[776,128]{1,0:T(8,128)(2,1)S(1)}, bf16[776,128]{1,0:T(8,128)(2,1)S(1)}, u32[]{:S(2)}, u32[]{:S(2)}) %collective-permute-start.5) | collective-permute-done | bytes 198688 | tf_op jit(solution)/shard_map/ppermute | solution.py:297
  217.5 2.7 %collective-permute-start.6 = (bf16[776,128]{1,0:T(8,128)(2,1)S(1)}, bf16[776,128]{1,0:T(8,128)(2,1)S(1)}, u32[]{:S(2)}, u32[]{:S(2)}) collective-permute-start(bf16[776,128]{1,0:T(8,128)(2,1)S(1)} %add_convert_fusion.1), channel_id=1, source_target_pairs={{0,4},{1,5},{2,6},{3,7},{4,0},{5,1},{6,2},{7,3},{8,12},{9,13},{10,... | collective-permute-start | bytes 595976 | tf_op jit(solution)/shard_map/ppermute | solution.py:297
  220.2 4.7 %collective-permute-done.2 = bf16[1024,128]{1,0:T(8,128)(2,1)S(1)} collective-permute-done((bf16[1024,128]{1,0:T(8,128)(2,1)S(1)}, bf16[1024,128]{1,0:T(8,128)(2,1)S(1)}, u32[]{:S(2)}, u32[]{:S(2)}) %collective-permute-start.2) | collective-permute-done | bytes 262176 | tf_op jit(solution)/shard_map/ppermute | solution.py:319
  224.9 3.3 %collective-permute-done.3 = bf16[1024,128]{1,0:T(8,128)(2,1)S(1)} collective-permute-done((bf16[1024,128]{1,0:T(8,128)(2,1)S(1)}, bf16[1024,128]{1,0:T(8,128)(2,1)S(1)}, u32[]{:S(2)}, u32[]{:S(2)}) %collective-permute-start.3) | collective-permute-done | bytes 262176 | tf_op jit(solution)/shard_map/ppermute | solution.py:318
  228.2 0.9 pad_maximum_fusion.1.back_ref
  229.0 9.0 %finish.1 = f32[4096,128]{1,0:T(8,128)} custom-call(s32[1,2048]{1,0:T(1,128)} %bitcast.31, bf16[2048,128]{1,0:T(8,128)(2,1)} %pad_maximum_fusion.1.back_ref, f32[6144,128]{1,0:T(8,128)} %get-tuple-element.17.dext_ref, f32[4096,128]{1,0:T(8,128)} %get-tuple-element.18.down_ref), custom_call_target="tpu_custom_call" | custom-call | tf_op jit(solution)/shard_map/finish/pallas_call | solution.py:273
  238.2 0.5 slice_bitcast_fusion
  238.7 0.7 fusion.3
  (29 shorter events, 0.7 us)
Async XLA Ops:
  1.4 7.1 %copy-start.3 = (s32[1,1,2,1024]{3,1,2,0:T(1,128)}, s32[1,1,2,1024]{3,1,2,0:T(1,128)S(1)}, u32[]{:S(2)}) copy-start(s32[1,1,2,1024]{3,1,2,0:T(1,128)S(1)} %copy.35) | copy-start | bytes 24580
  1.4 9.2 %copy-start.2 = (bf16[128,128]{1,0:T(8,128)(2,1)S(1)}, bf16[128,128]{1,0:T(8,128)(2,1)}, u32[]{:S(2)}) copy-start(bf16[128,128]{1,0:T(8,128)(2,1)} %w_msg_ref.1) | copy-start | bytes 98308
  1.4 9.3 %copy-start.1 = (s32[12,4096]{1,0:T(8,128)S(1)}, s32[12,4096]{1,0:T(8,128)}, u32[]{:S(2)}) copy-start(s32[12,4096]{1,0:T(8,128)} %param.16) | copy-start | bytes 589828
  1.4 9.3 %copy-start.4 = (s32[4096]{0:T(1024)S(1)}, s32[4096]{0:T(1024)}, u32[]{:S(2)}) copy-start(s32[4096]{0:T(1024)} %param.18) | copy-start | bytes 49156
  8.5 13.7 %collective-permute-start = (bf16[1024,128]{1,0:T(8,128)(2,1)S(1)}, bf16[1024,128]{1,0:T(8,128)(2,1)S(1)}, u32[]{:S(2)}, u32[]{:S(2)}) collective-permute-start(bf16[1024,128]{1,0:T(8,128)(2,1)S(1)} %get-tuple-element.23), channel_id=1, source_target_pairs={{0,1},{1,2},{2,3},{3,4},{4,5},{5,6},{6,7},{7,0},{8,9},{9,10},{10,1... | collective-permute-start | bytes 786440 | tf_op jit(solution)/shard_map/ppermute | solution.py:311
  10.1 12.1 %collective-permute-start.1 = (bf16[1024,128]{1,0:T(8,128)(2,1)S(1)}, bf16[1024,128]{1,0:T(8,128)(2,1)S(1)}, u32[]{:S(2)}, u32[]{:S(2)}) collective-permute-start(bf16[1024,128]{1,0:T(8,128)(2,1)S(1)} %get-tuple-element.24), channel_id=1, source_target_pairs={{1,0},{2,1},{3,2},{4,3},{5,4},{6,5},{7,6},{0,7},{9,8},{10,9},{11,1... | collective-permute-start | bytes 786440 | tf_op jit(solution)/shard_map/ppermute | solution.py:312
  10.8 11.4 %copy-start = (bf16[4096,128]{1,0:T(8,128)(2,1)S(1)}, bf16[4096,128]{1,0:T(8,128)(2,1)}, u32[]{:S(2)}) copy-start(bf16[4096,128]{1,0:T(8,128)(2,1)} %own_ref.1) | copy-start | bytes 3145732
  202.9 6.6 %collective-permute-start.4 = (bf16[776,128]{1,0:T(8,128)(2,1)S(1)}, bf16[776,128]{1,0:T(8,128)(2,1)S(1)}, u32[]{:S(2)}, u32[]{:S(2)}) collective-permute-start(bf16[776,128]{1,0:T(8,128)(2,1)S(1)} %pad_maximum_fusion.2), channel_id=1, source_target_pairs={{0,1},{1,0},{2,3},{3,2},{4,5},{5,4},{6,7},{7,6},{8,9},{9,8},{10,11... | collective-permute-start | bytes 595976 | tf_op jit(solution)/shard_map/ppermute | solution.py:297
  209.5 7.9 %collective-permute-start.5 = (bf16[776,128]{1,0:T(8,128)(2,1)S(1)}, bf16[776,128]{1,0:T(8,128)(2,1)S(1)}, u32[]{:S(2)}, u32[]{:S(2)}) collective-permute-start(bf16[776,128]{1,0:T(8,128)(2,1)S(1)} %add_convert_fusion.2), channel_id=1, source_target_pairs={{0,2},{1,3},{2,0},{3,1},{4,6},{5,7},{6,4},{7,5},{8,10},{9,11},{10,... | collective-permute-start | bytes 595976 | tf_op jit(solution)/shard_map/ppermute | solution.py:297
  209.7 15.2 %collective-permute-start.2 = (bf16[1024,128]{1,0:T(8,128)(2,1)S(1)}, bf16[1024,128]{1,0:T(8,128)(2,1)S(1)}, u32[]{:S(2)}, u32[]{:S(2)}) collective-permute-start(bf16[1024,128]{1,0:T(8,128)(2,1)S(1)} %get-tuple-element.21), channel_id=1, source_target_pairs={{0,1},{1,2},{2,3},{3,4},{4,5},{5,6},{6,7},{7,0},{8,9},{9,10},{10,1... | collective-permute-start | bytes 786440 | tf_op jit(solution)/shard_map/ppermute | solution.py:319
  214.0 14.1 %collective-permute-start.3 = (bf16[1024,128]{1,0:T(8,128)(2,1)S(1)}, bf16[1024,128]{1,0:T(8,128)(2,1)S(1)}, u32[]{:S(2)}, u32[]{:S(2)}) collective-permute-start(bf16[1024,128]{1,0:T(8,128)(2,1)S(1)} %get-tuple-element.22), channel_id=1, source_target_pairs={{1,0},{2,1},{3,2},{4,3},{5,4},{6,5},{7,6},{0,7},{9,8},{10,9},{11,1... | collective-permute-start | bytes 786440 | tf_op jit(solution)/shard_map/ppermute | solution.py:318
  217.5 20.6 %collective-permute-start.6 = (bf16[776,128]{1,0:T(8,128)(2,1)S(1)}, bf16[776,128]{1,0:T(8,128)(2,1)S(1)}, u32[]{:S(2)}, u32[]{:S(2)}) collective-permute-start(bf16[776,128]{1,0:T(8,128)(2,1)S(1)} %add_convert_fusion.1), channel_id=1, source_target_pairs={{0,4},{1,5},{2,6},{3,7},{4,0},{5,1},{6,2},{7,3},{8,12},{9,13},{10,... | collective-permute-start | bytes 595976 | tf_op jit(solution)/shard_map/ppermute | solution.py:297
where the time goes:
time: 240 us; the launch traced here: 239 us
  Pallas kernels  187 us (78%)
  waiting for transfers between devices  22.1 us (9%)
  local copies, waits for them, and re-layouts  12.1 us (5%)
  starting transfers between devices  10.7 us (4%)
  other arithmetic  6.99 us (3%)
    pallas_call x1, Pallas kernels, layer(): pl.pallas_call(functools.partial(layer_kernel, degree), grid=(blocks,), i...  178 us
    pallas_call x1, Pallas kernels, finish(): pl.pallas_call(finish_kernel, grid=(nodes // count,), in_specs=[pl.BlockS...  9.05 us
    ppermute x1, waiting for transfers between devices, on_device(): before = lax.ppermute(outbound[rim:], 'tile', up)  7.66 us
    gather x1, local copies, waits for them, and re-layouts, on_device(): outbound = node_latent[listing[0]]  7 us
    ppermute x3, waiting for transfers between devices, total_over(): other = lax.ppermute(value, axis, [(i, i ^ bit) for i in range(size)])  6.46 us
  transfers between devices with their start and end apart: 7, of which 5 were waited for; matrix products, arithmetic and copies ran while one was open for 3% of the time, Pallas kernels for 4%

commit v1 on v0

v1 whole, which is shorter than its diff:
```python
import functools

import jax
import jax.numpy as jnp
from jax import lax
from jax.experimental import pallas as pl
from jax.experimental.pallas import tpu as pltpu
from jax.sharding import PartitionSpec as P

CHUNK = 32
RING = 9
COPIES = 8
EMPTY = -1e4
PLAN = (
    "c1", ("s", 1), ("g", 1), "c2", ("s", 2), ("g", 2), "d1", ("s", 3), ("g", 3), "e1", ("s", 4), ("g", 4), "n2", ("s", 5), ("g", 5), "n1", ("s", 6), ("g", 6), "f1", ("s", 7), ("g", 7), ("s", 8), ("g", 8), "p1", ("s", 9), ("g", 9), "c1s", ("s", 10), ("g", 10), "d2", ("s", 11), ("g", 11), "e2", ("s", 12), ("g", 12), "n3", ("s", 13), ("g", 13), "n4", ("s", 14), ("g", 14), "n1s", ("s", 15), ("g", 15), "n5", ("s", 16), ("g", 16), ("s", 17), ("g", 17), "c3", ("s", 18), ("g", 18), "e3", ("s", 19), ("g", 19), ("s", 20), ("g", 20), "e3", ("s", 21), ("g", 21), ("s", 22), ("g", 22), "e3", ("s", 23), ("g", 23), ("s", 24), ("g", 24),
)
BF = jnp.bfloat16
F32 = jnp.float32


def mm(a, b):
    return jnp.dot(a, b, preferred_element_type=F32)


def mm_nt(a, b):
    return lax.dot_general(a, b, (((1,), (1,)), ((), ())), preferred_element_type=F32)


def mm_tn(a, b):
    return lax.dot_general(a, b, (((0,), (0,)), ((), ())), preferred_element_type=F32)


def sigmoid(x):
    return 0.5 * jnp.tanh(0.5 * x) + 0.5


def layer_kernel(
    degree,
    chunk,
    idx_ref,
    ct_ref,
    live_ref,
    ext_ref,
    w_src_ref,
    w_half_ref,
    w_dst_ref,
    w_back_ref,
    w_cent_ref,
    gain_ref,
    ebias_ref,
    w_self_ref,
    w_agg_ref,
    nbias_ref,
    w_out_ref,
    updated_ref,
    down_ref,
    halo_ref,
    gw_ref,
    gv_ref,
    table,
    hid,
    slope,
    yhat,
    rstd,
    dmsg,
    dhid,
    ysums,
    dycs,
    bases,
    sums,
    hid_new,
    slope_new,
    dps,
    pds,
    cents,
    pres,
    dinners,
    sbs,
    dobs,
    *accs,
):
    nodes, width = down_ref.shape
    listed = ext_ref.shape[0]
    copies = len(accs)
    steps = nodes // chunk
    edges = degree * chunk
    half = edges // 2
    groups = edges // 8

    table[pl.ds(0, listed), :] = mm(ext_ref[...], w_half_ref[...])
    table[pl.ds(listed, 8), :] = jnp.full((8, width), EMPTY, F32)
    for ref in (
        slope, yhat, rstd, dmsg, dhid, ysums, dycs, sums, hid, hid_new, slope_new, dps,
        cents, pres, dinners, sbs, dobs, *accs,
    ):
        ref[...] = jnp.zeros_like(ref)
    gw_ref[...] = jnp.zeros_like(gw_ref)

    ones = jnp.full((width, width), 1.0 / width, BF)
    zeros = jnp.zeros((width, width), BF)
    ones2 = jnp.concatenate(
        [jnp.concatenate([ones, zeros], 1), jnp.concatenate([zeros, ones], 1)], 0
    )
    at_row = lax.broadcasted_iota(jnp.int32, (8, width), 0)
    bit = [(at_row & b) != 0 for b in (1, 2, 4)]
    only = [at_row == j for j in range(8)]

    def rows_of(m):
        return pl.ds(pl.multiple_of(jnp.clip(m, 0, steps - 1) * chunk, chunk), chunk)

    def list_of(m):
        at = jnp.clip(m, 0, steps - 1)
        return lambda e: idx_ref.at[pl.ds(e * steps, steps)][at]

    def body(m, carry):
        gain = gain_ref[...]

        def slot(lag):
            return lax.rem(m + 2 * RING - lag, RING)

        v = {"pd": pds[...]}
        per = chunk // 8
        dpd = [None] * per
        idx0 = list_of(m)
        idx7 = list_of(m - 7)
        s7 = slot(7)

        def wide(x):
            return jnp.concatenate([x[:half], x[half:]], 1)

        def fold(x):
            return sum(x[i * 8 : i * 8 + 8] for i in range(1, per)) + x[:8]

        def gather(g):
            rows = [
                jnp.broadcast_to(table[pl.ds(idx0(g * 8 + j), 1), :], (8, width))
                for j in range(8)
            ]
            for b in bit:
                rows = [jnp.where(b, q, p) for p, q in zip(rows[::2], rows[1::2])]
            n = g % per
            z = rows[0] + v["pd"][n * 8 : n * 8 + 8]
            t = jnp.tanh(z)
            q = 1.0 + t
            h = z * q
            slope_new[pl.ds(g * 8, 8), :] = q + h * (1.0 - t)
            return h

        def scatter(chunks):
            for g in chunks:
                at = pl.ds(g * 8, 8)
                dx = dhid[at, :] * slope[s7, at, :]
                n = g % per
                dpd[n] = dx if dpd[n] is None else dpd[n] + dx
                for j in range(8):
                    acc = accs[(g * 8 + j) % copies]
                    to = pl.ds(idx7(g * 8 + j) + (8 - j), 8)
                    pltpu.store(acc.at[to, :], acc[to, :] + dx, mask=only[j])

        def c1():
            old = hid_new[...]
            hid[slot(1)] = old
            slope[slot(1)] = slope_new[...]
            v["c"] = mm(wide(old), w_cent_ref[...])

        def c1s():
            cents[...] = v["c"]

        def c2():
            v["c2"] = cents[...]
            v["var"] = mm((v["c2"] * v["c2"]).astype(BF), ones2)

        def c3():
            r = lax.rsqrt(v["var"] + 1e-5)
            y = v["c2"] * r
            yhat[slot(2)] = y
            rstd[slot(2)] = r
            ys = y[:, :width] + y[:, width:]
            ysums[slot(2)] = (
                sum(ys[i * chunk : (i + 1) * chunk] for i in range(1, degree // 2))
                + ys[:chunk]
            )

        def n1():
            at = rows_of(m - 3)
            own = ext_ref[at, :]
            sb = (ysums[slot(3)] * gain).astype(BF)
            v["pre"] = (
                mm(own, w_self_ref[...]) + mm(sb, w_agg_ref[...]) + nbias_ref[...]
            )
            inside = jnp.logical_and(m >= 3, m < steps + 3).astype(F32)
            dob = (inside * live_ref[at, :].astype(F32) * ct_ref[at, :]).astype(BF)
            v["dinner"] = mm_nt(dob, w_out_ref[...])
            v["sb"] = sb
            v["dob"] = dob

        def n1s():
            pres[...] = v["pre"]
            dinners[...] = v["dinner"]
            sbs[...] = v["sb"]
            dobs[...] = v["dob"]

        def n2():
            pre = pres[...]
            sg = sigmoid(pre)
            u = pre * sg
            v["ub"] = u.astype(BF)
            v["dpre"] = dinners[...] * (sg + u - u * sg)
            v["dpb"] = v["dpre"].astype(BF)
            v["dsum"] = mm_nt(v["dpb"], w_agg_ref[...])

        def n3():
            at = rows_of(m - 4)
            own = ext_ref[at, :]
            updated_ref[at, :] = (
                own.astype(F32)
                + live_ref[at, :].astype(F32) * mm(v["ub"], w_out_ref[...])
            ).astype(BF)
            bases[slot(4)] = ct_ref[at, :] + mm_nt(v["dpb"], w_self_ref[...])
            sums[2] += fold(v["dpre"])

        def n4():
            gw_ref[3] += mm_tn(ext_ref[rows_of(m - 4), :], v["dpb"])
            gw_ref[4] += mm_tn(sbs[...], v["dpb"])
            gw_ref[5] += mm_tn(v["ub"], dobs[...])

        def n5():
            dy = v["dsum"] * gain
            dycs[...] = dy - jnp.mean(dy, axis=1, keepdims=True)
            sums[0] += fold(v["dsum"] * ysums[slot(4)])

        def d1():
            d = dycs[...]
            d = jnp.concatenate([d] * (degree // 2), 0)
            v["d"] = jnp.concatenate([d, d], 1)
            v["t"] = mm((v["d"] * yhat[slot(5)]).astype(BF), ones2)

        def d2():
            y = yhat[slot(5)]
            dm = (rstd[slot(5)] * (v["d"] - y * v["t"])).astype(BF)
            dmsg[pl.ds(0, half), :] = dm[:, :width]
            dmsg[pl.ds(half, half), :] = dm[:, width:]

        def e1():
            v["dm"] = dmsg[...]
            v["dh"] = mm(wide(v["dm"]), w_back_ref[...])

        def e2():
            gw_ref[2] += mm_tn(hid[slot(6)], v["dm"])

        def e3(first, last):
            for g in range(first, last):
                if g * 8 < half:
                    part = v["dh"][g * 8 : g * 8 + 8, :width]
                else:
                    part = v["dh"][g * 8 - half : g * 8 - half + 8, width:]
                dhid[pl.ds(g * 8, 8), :] = part

        def f1():
            at = rows_of(m - 8)
            dp = dps[...]
            dpdb = dp.astype(BF)
            down_ref[at, :] = bases[slot(8)] + mm_nt(dpdb, w_dst_ref[...])
            gw_ref[1] += mm_tn(ext_ref[at, :], dpdb)
            sums[1] += fold(dp)

        def p1():
            own = ext_ref[rows_of(m + 1), :]
            pds[...] = 0.5 * (mm(own, w_dst_ref[...]) + ebias_ref[...])

        stages = dict(
            c1=c1, c1s=c1s, c2=c2, c3=c3, n1=n1, n1s=n1s, n2=n2, n3=n3, n4=n4, n5=n5,
            d1=d1, d2=d2, e1=e1, e2=e2, f1=f1, p1=p1,
        )
        done = written = taken = 0
        for item in PLAN:
            if item == "e3":
                e3(written, done)
                written = done
            elif isinstance(item, str):
                stages[item]()
            else:
                kind, last = item[0], groups * item[1] // 24
                if kind == "s":
                    scatter(range(done, last))
                    done = last
                else:
                    for g in range(taken, last, 2):
                        pair = jnp.concatenate([gather(g), gather(g + 1)], 0)
                        hid_new[pl.ds(g * 8, 16), :] = pair.astype(BF)
                    taken = last
        e3(written, groups)
        dps[...] = jnp.concatenate(dpd, 0)
        return carry

    pds[...] = 0.5 * (mm(ext_ref[pl.ds(0, chunk), :], w_dst_ref[...]) + ebias_ref[...])
    lax.fori_loop(0, steps + 8, body, 0)

    gv_ref[...] = jnp.concatenate(
        [jnp.sum(sums[i], axis=0, keepdims=True) for i in range(3)]
        + [jnp.zeros((5, width), F32)],
        0,
    )
    dproj = accs[0][pl.ds(8, listed), :]
    for acc in accs[1:]:
        dproj = dproj + acc[pl.ds(8, listed), :]
    dpb = dproj.astype(BF)
    dext = mm_nt(dpb, w_src_ref[...])
    down_ref[...] += dext[:nodes]
    halo_ref[...] = dext[nodes:].astype(BF)
    gw_ref[0] = mm_tn(ext_ref[...], dpb)


def diagonal(w):
    zero = jnp.zeros_like(w)
    return jnp.concatenate(
        [jnp.concatenate([w, zero], 1), jnp.concatenate([zero, w], 1)], 0
    )


def layer(extended, cotangent, neighbours, node_mask, weights):
    w_src, w_dst, w_msg, edge_gain, edge_bias, w_self, w_agg, node_bias, w_out = weights
    degree, nodes = neighbours.shape
    width = cotangent.shape[1]
    listed = extended.shape[0]
    chunk = min(CHUNK, nodes)
    steps = nodes // chunk
    edges = degree * chunk
    idx = jnp.where(neighbours < 0, listed, neighbours)
    idx = idx.reshape(degree, steps, chunk).transpose(0, 2, 1).reshape(-1)
    live = jnp.broadcast_to(node_mask.astype(BF)[:, None], (nodes, width))
    w32 = w_msg.astype(F32)
    w_cent = (w32 - jnp.mean(w32, axis=1, keepdims=True)).astype(BF)
    half = jnp.asarray(0.5, BF)
    vmem = pl.BlockSpec(memory_space=pltpu.VMEM)
    return pl.pallas_call(
        functools.partial(layer_kernel, degree, chunk),
        in_specs=[pl.BlockSpec(memory_space=pltpu.SMEM)] + [vmem] * 14,
        out_specs=[vmem] * 5,
        out_shape=[
            jax.ShapeDtypeStruct((nodes, width), BF),
            jax.ShapeDtypeStruct((nodes, width), F32),
            jax.ShapeDtypeStruct((listed - nodes, width), BF),
            jax.ShapeDtypeStruct((6, width, width), F32),
            jax.ShapeDtypeStruct((8, width), F32),
        ],
        scratch_shapes=[
            pltpu.VMEM((listed + 8, width), F32),
            pltpu.VMEM((RING, edges, width), BF),
            pltpu.VMEM((RING, edges, width), F32),
            pltpu.VMEM((RING, edges // 2, 2 * width), F32),
            pltpu.VMEM((RING, edges // 2, 2 * width), F32),
            pltpu.VMEM((edges, width), BF),
            pltpu.VMEM((edges, width), F32),
            pltpu.VMEM((RING, chunk, width), F32),
            pltpu.VMEM((chunk, width), F32),
            pltpu.VMEM((RING, chunk, width), F32),
            pltpu.VMEM((3, 8, width), F32),
            pltpu.VMEM((edges, width), BF),
            pltpu.VMEM((edges, width), F32),
            pltpu.VMEM((chunk, width), F32),
            pltpu.VMEM((chunk, width), F32),
            pltpu.VMEM((edges // 2, 2 * width), F32),
            pltpu.VMEM((chunk, width), F32),
            pltpu.VMEM((chunk, width), F32),
            pltpu.VMEM((chunk, width), BF),
            pltpu.VMEM((chunk, width), BF),
        ]
        + [pltpu.VMEM((listed + 24, width), F32)] * COPIES,
        compiler_params=pltpu.CompilerParams(vmem_limit_bytes=60 * 2**20),
        name="layer",
    )(
        idx,
        cotangent,
        live,
        extended,
        w_src,
        w_src * half,
        w_dst,
        diagonal(w_msg.T * half),
        diagonal(w_cent),
        edge_gain[None],
        edge_bias[None],
        w_self,
        w_agg,
        node_bias[None],
        w_out,
    )


def finish_kernel(list_ref, back_ref, down_ref, out_ref):
    count = out_ref.shape[0]
    first = pl.program_id(0) * count
    span = list_ref.shape[1]
    here = lax.broadcasted_iota(jnp.int32, (count, span), 0) + first
    hit = jnp.where(here == list_ref[...], 1.0, 0.0).astype(BF)
    out_ref[...] = down_ref[...] + mm(hit, back_ref[...])


def finish(listing, back, down):
    nodes, width = down.shape
    count = min(512, nodes)
    rowed = pl.BlockSpec((count, width), lambda i: (i, 0))
    return pl.pallas_call(
        finish_kernel,
        grid=(nodes // count,),
        in_specs=[
            pl.BlockSpec((1, listing.shape[1]), lambda i: (0, 0)),
            pl.BlockSpec(back.shape, lambda i: (0, 0)),
            rowed,
        ],
        out_specs=rowed,
        out_shape=jax.ShapeDtypeStruct((nodes, width), F32),
        compiler_params=pltpu.CompilerParams(
            dimension_semantics=("arbitrary",), vmem_limit_bytes=60 * 2**20
        ),
        name="finish",
    )(listing, back, down)


def total_over(value, axis):
    size = lax.axis_size(axis)
    if size & (size - 1):
        return lax.psum(value, axis)
    bit = 1
    while bit < size:
        other = lax.ppermute(value, axis, [(i, i ^ bit) for i in range(size)])
        value = (value.astype(F32) + other.astype(F32)).astype(BF)
        bit *= 2
    return value


def on_device(node_latent, cotangent, neighbours, send_rows, node_mask, *weights):
    nodes = node_latent.shape[0]
    rim = send_rows.shape[2]
    size = lax.axis_size("tile")
    up = [(i, (i + 1) % size) for i in range(size)]
    down = [(j, i) for i, j in up]
    listing = send_rows.reshape(1, 2 * rim)
    outbound = node_latent[listing[0]]
    before = lax.ppermute(outbound[rim:], "tile", up)
    after = lax.ppermute(outbound[:rim], "tile", down)
    extended = jnp.concatenate([node_latent, before, after], axis=0)
    updated, down_grad, halo, gw, gv = layer(
        extended, cotangent, neighbours, node_mask, weights
    )
    to_below = lax.ppermute(halo[:rim], "tile", down)
    to_above = lax.ppermute(halo[rim:], "tile", up)
    back = jnp.concatenate([to_above, to_below], axis=0)
    packed = jnp.concatenate([gw.reshape(-1, gw.shape[2]), gv], axis=0).astype(BF)
    packed = total_over(packed, "tile").astype(F32)
    latent_grad = finish(listing, back, down_grad)
    packed = packed * (nodes * size) ** (-0.5)
    width = gw.shape[2]
    mats = [packed[i * width : (i + 1) * width] for i in range(6)]
    vecs = [packed[6 * width + i] for i in range(3)]
    return (
        updated,
        latent_grad,
        mats[0],
        mats[1],
        mats[2],
        vecs[0],
        vecs[1],
        mats[3],
        mats[4],
        vecs[2],
        mats[5],
    )


def solution(mesh):
    rowed, shared = P(("scene", "tile"), None), P()
    in_specs = (
        rowed,
        rowed,
        P(None, ("scene", "tile")),
        P(("scene", "tile"), None, None),
        P(("scene", "tile")),
    ) + (shared,) * 9
    mat, vec = P("scene", None), P("scene")
    out_specs = (rowed, rowed, mat, mat, mat, vec, vec, mat, mat, vec, mat)
    return jax.shard_map(
        on_device, mesh=mesh, in_specs=in_specs, out_specs=out_specs, check_vma=False
    )
```

time: 240 us -> 172 us (0.72)
  Pallas kernels: 187 us -> 117 us
  waiting for transfers between devices: 22.1 us -> 25.3 us
    pallas_call x1, Pallas kernels: 178 us -> 108 us  [layer(): pl.pallas_call(functools.partial(layer_kernel, degree, chunk), in_specs=[...]
  transfers between devices with their start and end apart: 7 -> 7, of which waited for: 5 -> 5; matrix products, arithmetic and copies ran while one was open for 3% -> 3% of each run, Pallas kernels for 4% -> 5%
where the time goes in v1:
time: 172 us
  Pallas kernels  117 us (68%)
  waiting for transfers between devices  25.3 us (15%)
  local copies, waits for them, and re-layouts  13.8 us (8%)
  starting transfers between devices  10.5 us (6%)
  other arithmetic  4.99 us (3%)
    pallas_call x1, Pallas kernels, layer(): pl.pallas_call(functools.partial(layer_kernel, degree, chunk), in_specs=[...  108 us
    pallas_call x1, Pallas kernels, finish(): pl.pallas_call(finish_kernel, grid=(nodes // count,), in_specs=[pl.BlockS...  8.68 us
    ppermute x1, waiting for transfers between devices, on_device(): before = lax.ppermute(outbound[rim:], 'tile', up)  8.46 us
    ppermute x3, waiting for transfers between devices, total_over(): other = lax.ppermute(value, axis, [(i, i ^ bit) for i in range(size)])  7.11 us
    gather x1, local copies, waits for them, and re-layouts, on_device(): outbound = node_latent[listing[0]]  7 us
    ppermute x1, waiting for transfers between devices, on_device(): to_above = lax.ppermute(halo[rim:], 'tile', up)  6.47 us
    ppermute x1, starting transfers between devices, on_device(): to_above = lax.ppermute(halo[rim:], 'tile', up)  4.36 us
    ppermute x3, starting transfers between devices, total_over(): other = lax.ppermute(value, axis, [(i, i ^ bit) for i in range(size)])  4.05 us
  transfers between devices with their start and end apart: 7, of which 5 were waited for; matrix products, arithmetic and copies ran while one was open for 3% of the time, Pallas kernels for 5%

profile of v1, /device:TPU:14, one launch (start us, length us, event | category | flops | bytes accessed | tf_op | source)
XLA Modules:
  0.0 172.0 jit_solution(536532136557878880)
XLA Ops:
  0.6 0.7 copy.32
  1.4 7.0 %gather_fusion = bf16[2048,128]{1,0:T(8,128)(2,1)S(1)} fusion(bf16[4096,128]{1,0:T(8,128)(2,1)} %param.14, s32[2048]{0:T(1024)S(1)} %broadcast_clamp_fusion), kind=kCustom, calls=%fused_computation | custom fusion | bytes 1056768 | tf_op jit(solution)/shard_map/gather | solution.py:440
  8.5 1.6 collective-permute-start
  11.1 0.7 copy.31.w_half_ref
  12.1 0.9 copy.28
  13.0 0.8 fusion.4
  13.8 8.5 %collective-permute-done = bf16[1024,128]{1,0:T(8,128)(2,1)S(1)} collective-permute-done((bf16[1024,128]{1,0:T(8,128)(2,1)S(1)}, bf16[1024,128]{1,0:T(8,128)(2,1)S(1)}, u32[]{:S(2)}, u32[]{:S(2)}) %collective-permute-start) | collective-permute-done | bytes 262176 | tf_op jit(solution)/shard_map/ppermute | solution.py:441
  22.2 1.2 pad_maximum_fusion.ext_ref
  23.5 1.6 broadcast_in_dim.22.live_ref
  25.1 107.8 %layer.1 = (bf16[4096,128]{1,0:T(8,128)(2,1)}, f32[4096,128]{1,0:T(8,128)}, bf16[2048,128]{1,0:T(8,128)(2,1)}, f32[6,128,128]{2,1,0:T(8,128)}, f32[8,128]{1,0:T(8,128)}) custom-call(s32[49152]{0:T(1024)} %bitcast.23, f32[4096,128]{1,0:T(8,128)} %ct_ref.1, bf16[4096,128]{1,0:T(8,128)(2,1)} %broadcast_in_dim.22.live_ref, ...), custom_call_target="tpu_custom_call" | custom-call | tf_op jit(solution)/shard_map/layer/pallas_call | solution.py:336
  132.9 0.7 convert.8
  133.6 1.0 convert.7
  134.6 1.5 collective-permute-start.4
  136.1 5.2 %collective-permute-done.4 = bf16[776,128]{1,0:T(8,128)(2,1)S(1)} collective-permute-done((bf16[776,128]{1,0:T(8,128)(2,1)S(1)}, bf16[776,128]{1,0:T(8,128)(2,1)S(1)}, u32[]{:S(2)}, u32[]{:S(2)}) %collective-permute-start.4) | collective-permute-done | bytes 198688 | tf_op jit(solution)/shard_map/ppermute | solution.py:427
  141.4 1.1 fusion.7
  142.5 4.4 %collective-permute-start.2 = (bf16[1024,128]{1,0:T(8,128)(2,1)S(1)}, bf16[1024,128]{1,0:T(8,128)(2,1)S(1)}, u32[]{:S(2)}, u32[]{:S(2)}) collective-permute-start(bf16[1024,128]{1,0:T(8,128)(2,1)S(1)} %get-tuple-element.21), channel_id=1, source_target_pairs={{0,1},{1,2},{2,3},{3,4},{4,5},{5,6},{6,7},{7,0},{8,9},{9,10},{10,1... | collective-permute-start | bytes 786440 | tf_op jit(solution)/shard_map/ppermute | solution.py:448
  146.9 1.9 %collective-permute-done.5 = bf16[776,128]{1,0:T(8,128)(2,1)S(1)} collective-permute-done((bf16[776,128]{1,0:T(8,128)(2,1)S(1)}, bf16[776,128]{1,0:T(8,128)(2,1)S(1)}, u32[]{:S(2)}, u32[]{:S(2)}) %collective-permute-start.5) | collective-permute-done | bytes 198688 | tf_op jit(solution)/shard_map/ppermute | solution.py:427
  148.9 2.5 %collective-permute-start.6 = (bf16[776,128]{1,0:T(8,128)(2,1)S(1)}, bf16[776,128]{1,0:T(8,128)(2,1)S(1)}, u32[]{:S(2)}, u32[]{:S(2)}) collective-permute-start(bf16[776,128]{1,0:T(8,128)(2,1)S(1)} %add_convert_fusion.1), channel_id=1, source_target_pairs={{0,4},{1,5},{2,6},{3,7},{4,0},{5,1},{6,2},{7,3},{8,12},{9,13},{10,... | collective-permute-start | bytes 595976 | tf_op jit(solution)/shard_map/ppermute | solution.py:427
  151.4 6.5 %collective-permute-done.2 = bf16[1024,128]{1,0:T(8,128)(2,1)S(1)} collective-permute-done((bf16[1024,128]{1,0:T(8,128)(2,1)S(1)}, bf16[1024,128]{1,0:T(8,128)(2,1)S(1)}, u32[]{:S(2)}, u32[]{:S(2)}) %collective-permute-start.2) | collective-permute-done | bytes 262176 | tf_op jit(solution)/shard_map/ppermute | solution.py:448
  157.8 3.3 %collective-permute-done.3 = bf16[1024,128]{1,0:T(8,128)(2,1)S(1)} collective-permute-done((bf16[1024,128]{1,0:T(8,128)(2,1)S(1)}, bf16[1024,128]{1,0:T(8,128)(2,1)S(1)}, u32[]{:S(2)}, u32[]{:S(2)}) %collective-permute-start.3) | collective-permute-done | bytes 262176 | tf_op jit(solution)/shard_map/ppermute | solution.py:447
  161.1 0.9 pad_maximum_fusion.1.back_ref
  162.0 8.7 %finish.1 = f32[4096,128]{1,0:T(8,128)} custom-call(s32[1,2048]{1,0:T(1,128)} %bitcast.25, bf16[2048,128]{1,0:T(8,128)(2,1)} %pad_maximum_fusion.1.back_ref, f32[4096,128]{1,0:T(8,128)} %get-tuple-element.18.down_ref), custom_call_target="tpu_custom_call" | custom-call | tf_op jit(solution)/shard_map/finish/pallas_call | solution.py:404
  170.7 0.5 slice_bitcast_fusion
  171.2 0.7 fusion.9
  (34 shorter events, 1.5 us)
Async XLA Ops:
  1.4 7.1 %copy-start.4 = (s32[1,1,2,1024]{3,1,2,0:T(1,128)}, s32[1,1,2,1024]{3,1,2,0:T(1,128)S(1)}, u32[]{:S(2)}) copy-start(s32[1,1,2,1024]{3,1,2,0:T(1,128)S(1)} %copy.32) | copy-start | bytes 24580
  1.4 9.2 %copy-start.1 = (bf16[128,128]{1,0:T(8,128)(2,1)S(1)}, bf16[128,128]{1,0:T(8,128)(2,1)}, u32[]{:S(2)}) copy-start(bf16[128,128]{1,0:T(8,128)(2,1)} %param.21) | copy-start | bytes 98308
  1.4 9.4 %copy-start.5 = (s32[4096]{0:T(1024)S(1)}, s32[4096]{0:T(1024)}, u32[]{:S(2)}) copy-start(s32[4096]{0:T(1024)} %param.18) | copy-start | bytes 49156
  1.4 9.5 %copy-start.3 = (bf16[128,128]{1,0:T(8,128)(2,1)S(1)}, bf16[128,128]{1,0:T(8,128)(2,1)}, u32[]{:S(2)}) copy-start(bf16[128,128]{1,0:T(8,128)(2,1)} %w_src_ref.1) | copy-start | bytes 98308
  1.4 10.4 %copy-start.2 = (s32[12,4096]{1,0:T(8,128)S(1)}, s32[12,4096]{1,0:T(8,128)}, u32[]{:S(2)}) copy-start(s32[12,4096]{1,0:T(8,128)} %param.16) | copy-start | bytes 589828
  8.5 13.8 %copy-start = (bf16[4096,128]{1,0:T(8,128)(2,1)S(1)}, bf16[4096,128]{1,0:T(8,128)(2,1)}, u32[]{:S(2)}) copy-start(bf16[4096,128]{1,0:T(8,128)(2,1)} %param.14) | copy-start | bytes 3145732
  8.5 13.7 %collective-permute-start = (bf16[1024,128]{1,0:T(8,128)(2,1)S(1)}, bf16[1024,128]{1,0:T(8,128)(2,1)S(1)}, u32[]{:S(2)}, u32[]{:S(2)}) collective-permute-start(bf16[1024,128]{1,0:T(8,128)(2,1)S(1)} %get-tuple-element.23), channel_id=1, source_target_pairs={{0,1},{1,2},{2,3},{3,4},{4,5},{5,6},{6,7},{7,0},{8,9},{9,10},{10,1... | collective-permute-start | bytes 786440 | tf_op jit(solution)/shard_map/ppermute | solution.py:441
  10.1 12.1 %collective-permute-start.1 = (bf16[1024,128]{1,0:T(8,128)(2,1)S(1)}, bf16[1024,128]{1,0:T(8,128)(2,1)S(1)}, u32[]{:S(2)}, u32[]{:S(2)}) collective-permute-start(bf16[1024,128]{1,0:T(8,128)(2,1)S(1)} %get-tuple-element.24), channel_id=1, source_target_pairs={{1,0},{2,1},{3,2},{4,3},{5,4},{6,5},{7,6},{0,7},{9,8},{10,9},{11,1... | collective-permute-start | bytes 786440 | tf_op jit(solution)/shard_map/ppermute | solution.py:442
  134.6 6.7 %collective-permute-start.4 = (bf16[776,128]{1,0:T(8,128)(2,1)S(1)}, bf16[776,128]{1,0:T(8,128)(2,1)S(1)}, u32[]{:S(2)}, u32[]{:S(2)}) collective-permute-start(bf16[776,128]{1,0:T(8,128)(2,1)S(1)} %pad_maximum_fusion.2), channel_id=1, source_target_pairs={{0,1},{1,0},{2,3},{3,2},{4,5},{5,4},{6,7},{7,6},{8,9},{9,8},{10,11... | collective-permute-start | bytes 595976 | tf_op jit(solution)/shard_map/ppermute | solution.py:427
  141.4 7.5 %collective-permute-start.5 = (bf16[776,128]{1,0:T(8,128)(2,1)S(1)}, bf16[776,128]{1,0:T(8,128)(2,1)S(1)}, u32[]{:S(2)}, u32[]{:S(2)}) collective-permute-start(bf16[776,128]{1,0:T(8,128)(2,1)S(1)} %add_convert_fusion.2), channel_id=1, source_target_pairs={{0,2},{1,3},{2,0},{3,1},{4,6},{5,7},{6,4},{7,5},{8,10},{9,11},{10,... | collective-permute-start | bytes 595976 | tf_op jit(solution)/shard_map/ppermute | solution.py:427
  142.5 15.3 %collective-permute-start.2 = (bf16[1024,128]{1,0:T(8,128)(2,1)S(1)}, bf16[1024,128]{1,0:T(8,128)(2,1)S(1)}, u32[]{:S(2)}, u32[]{:S(2)}) collective-permute-start(bf16[1024,128]{1,0:T(8,128)(2,1)S(1)} %get-tuple-element.21), channel_id=1, source_target_pairs={{0,1},{1,2},{2,3},{3,4},{4,5},{5,6},{6,7},{7,0},{8,9},{9,10},{10,1... | collective-permute-start | bytes 786440 | tf_op jit(solution)/shard_map/ppermute | solution.py:448
  146.9 14.2 %collective-permute-start.3 = (bf16[1024,128]{1,0:T(8,128)(2,1)S(1)}, bf16[1024,128]{1,0:T(8,128)(2,1)S(1)}, u32[]{:S(2)}, u32[]{:S(2)}) collective-permute-start(bf16[1024,128]{1,0:T(8,128)(2,1)S(1)} %get-tuple-element.22), channel_id=1, source_target_pairs={{1,0},{2,1},{3,2},{4,3},{5,4},{6,5},{7,6},{0,7},{9,8},{10,9},{11,1... | collective-permute-start | bytes 786440 | tf_op jit(solution)/shard_map/ppermute | solution.py:447
  148.9 21.8 %collective-permute-start.6 = (bf16[776,128]{1,0:T(8,128)(2,1)S(1)}, bf16[776,128]{1,0:T(8,128)(2,1)S(1)}, u32[]{:S(2)}, u32[]{:S(2)}) collective-permute-start(bf16[776,128]{1,0:T(8,128)(2,1)S(1)} %add_convert_fusion.1), channel_id=1, source_target_pairs={{0,4},{1,5},{2,6},{3,7},{4,0},{5,1},{6,2},{7,3},{8,12},{9,13},{10,... | collective-permute-start | bytes 595976 | tf_op jit(solution)/shard_map/ppermute | solution.py:427

commit v2 on v1

--- a/solution.py
+++ b/solution.py
@@ -8,14 +8,15 @@
 from jax.sharding import PartitionSpec as P
 
 CHUNK = 32
-RING = 9
+RING = 8
 COPIES = 8
 EMPTY = -1e4
 PLAN = (
-    "c1", ("s", 1), ("g", 1), "c2", ("s", 2), ("g", 2), "d1", ("s", 3), ("g", 3), "e1", ("s", 4), ("g", 4), "n2", ("s", 5), ("g", 5), "n1", ("s", 6), ("g", 6), "f1", ("s", 7), ("g", 7), ("s", 8), ("g", 8), "p1", ("s", 9), ("g", 9), "c1s", ("s", 10), ("g", 10), "d2", ("s", 11), ("g", 11), "e2", ("s", 12), ("g", 12), "n3", ("s", 13), ("g", 13), "n4", ("s", 14), ("g", 14), "n1s", ("s", 15), ("g", 15), "n5", ("s", 16), ("g", 16), ("s", 17), ("g", 17), "c3", ("s", 18), ("g", 18), "e3", ("s", 19), ("g", 19), ("s", 20), ("g", 20), "e3", ("s", 21), ("g", 21), ("s", 22), ("g", 22), "e3", ("s", 23), ("g", 23), ("s", 24), ("g", 24),
+    "c1", "c2", ("s", 1), ("g", 1), "d1", "e1", ("s", 2), ("g", 2), "n2", "n1", ("s", 3), ("g", 3), "f1", "p1", ("s", 4), ("g", 4), ("s", 5), ("g", 5), "c1s", ("s", 6), ("g", 6), ("s", 7), ("g", 7), "d2", ("s", 8), ("g", 8), "e2", ("s", 9), ("g", 9), "n3", ("s", 10), ("g", 10), "n4", ("s", 11), ("g", 11), "n1s", ("s", 12), ("g", 12), "n5", ("s", 13), ("g", 13), "c3", ("s", 14), ("g", 14), "e3", ("s", 15), ("g", 15), ("s", 16), ("g", 16), "e3", ("s", 17), ("g", 17), ("s", 18), ("g", 18), ("s", 19), ("g", 19), ("s", 20), ("g", 20), ("s", 21), ("g", 21), ("s", 22), ("g", 22), ("s", 23), ("g", 23), "e3", ("s", 24), ("g", 24),
 )
 BF = jnp.bfloat16
 F32 = jnp.float32
+MESH = pl.DeviceIdType.MESH
 
 
 def mm(a, b):
@@ -39,8 +40,9 @@
     chunk,
     idx_ref,
     ct_ref,
-    live_ref,
-    ext_ref,
+    mask_ref,
+    own_ref,
+    rim_ref,
     w_src_ref,
     w_half_ref,
     w_dst_ref,
@@ -77,17 +79,19 @@
     dinners,
     sbs,
     dobs,
+    live_ref,
     *accs,
 ):
     nodes, width = down_ref.shape
-    listed = ext_ref.shape[0]
+    listed = nodes + rim_ref.shape[0]
     copies = len(accs)
     steps = nodes // chunk
     edges = degree * chunk
     half = edges // 2
     groups = edges // 8
 
-    table[pl.ds(0, listed), :] = mm(ext_ref[...], w_half_ref[...])
+    table[pl.ds(0, nodes), :] = mm(own_ref[...], w_half_ref[...])
+    table[pl.ds(nodes, listed - nodes), :] = mm(rim_ref[...], w_half_ref[...])
     table[pl.ds(listed, 8), :] = jnp.full((8, width), EMPTY, F32)
     for ref in (
         slope, yhat, rstd, dmsg, dhid, ysums, dycs, sums, hid, hid_new, slope_new, dps,
@@ -101,6 +105,15 @@
     ones2 = jnp.concatenate(
         [jnp.concatenate([ones, zeros], 1), jnp.concatenate([zeros, ones], 1)], 0
     )
+    lanes = mask_ref.shape[1]
+    eye = lax.broadcasted_iota(jnp.int32, (lanes, lanes), 0) == (
+        lax.broadcasted_iota(jnp.int32, (lanes, lanes), 1)
+    )
+    every = jnp.ones((lanes, width), BF)
+    for g in range(nodes // lanes):
+        row = mask_ref[g : g + 1, :].astype(F32)
+        spread = jnp.where(eye, jnp.broadcast_to(row, (lanes, lanes)), 0.0)
+        live_ref[pl.ds(g * lanes, lanes), :] = mm(spread.astype(BF), every).astype(BF)
     at_row = lax.broadcasted_iota(jnp.int32, (8, width), 0)
     bit = [(at_row & b) != 0 for b in (1, 2, 4)]
     only = [at_row == j for j in range(8)]
@@ -115,8 +128,8 @@
     def body(m, carry):
         gain = gain_ref[...]
 
-        def slot(lag):
-            return lax.rem(m + 2 * RING - lag, RING)
+        def slot(lag, ring=RING):
+            return lax.rem(m + 2 * ring - lag, ring)
 
         v = {"pd": pds[...]}
         per = chunk // 8
@@ -173,8 +186,8 @@
         def c3():
             r = lax.rsqrt(v["var"] + 1e-5)
             y = v["c2"] * r
-            yhat[slot(2)] = y
-            rstd[slot(2)] = r
+            yhat[slot(2, 4)] = y
+            rstd[slot(2, 4)] = r
             ys = y[:, :width] + y[:, width:]
             ysums[slot(2)] = (
                 sum(ys[i * chunk : (i + 1) * chunk] for i in range(1, degree // 2))
@@ -183,7 +196,7 @@
 
         def n1():
             at = rows_of(m - 3)
-            own = ext_ref[at, :]
+            own = own_ref[at, :]
             sb = (ysums[slot(3)] * gain).astype(BF)
             v["pre"] = (
                 mm(own, w_self_ref[...]) + mm(sb, w_agg_ref[...]) + nbias_ref[...]
@@ -211,16 +224,16 @@
 
         def n3():
             at = rows_of(m - 4)
-            own = ext_ref[at, :]
+            own = own_ref[at, :]
             updated_ref[at, :] = (
                 own.astype(F32)
                 + live_ref[at, :].astype(F32) * mm(v["ub"], w_out_ref[...])
             ).astype(BF)
-            bases[slot(4)] = ct_ref[at, :] + mm_nt(v["dpb"], w_self_ref[...])
+            bases[slot(4, 5)] = ct_ref[at, :] + mm_nt(v["dpb"], w_self_ref[...])
             sums[2] += fold(v["dpre"])
 
         def n4():
-            gw_ref[3] += mm_tn(ext_ref[rows_of(m - 4), :], v["dpb"])
+            gw_ref[3] += mm_tn(own_ref[rows_of(m - 4), :], v["dpb"])
             gw_ref[4] += mm_tn(sbs[...], v["dpb"])
             gw_ref[5] += mm_tn(v["ub"], dobs[...])
 
@@ -233,11 +246,11 @@
             d = dycs[...]
             d = jnp.concatenate([d] * (degree // 2), 0)
             v["d"] = jnp.concatenate([d, d], 1)
-            v["t"] = mm((v["d"] * yhat[slot(5)]).astype(BF), ones2)
+            v["t"] = mm((v["d"] * yhat[slot(5, 4)]).astype(BF), ones2)
 
         def d2():
-            y = yhat[slot(5)]
-            dm = (rstd[slot(5)] * (v["d"] - y * v["t"])).astype(BF)
+            y = yhat[slot(5, 4)]
+            dm = (rstd[slot(5, 4)] * (v["d"] - y * v["t"])).astype(BF)
             dmsg[pl.ds(0, half), :] = dm[:, :width]
             dmsg[pl.ds(half, half), :] = dm[:, width:]
 
@@ -260,12 +273,12 @@
             at = rows_of(m - 8)
             dp = dps[...]
             dpdb = dp.astype(BF)
-            down_ref[at, :] = bases[slot(8)] + mm_nt(dpdb, w_dst_ref[...])
-            gw_ref[1] += mm_tn(ext_ref[at, :], dpdb)
+            down_ref[at, :] = bases[slot(8, 5)] + mm_nt(dpdb, w_dst_ref[...])
+            gw_ref[1] += mm_tn(own_ref[at, :], dpdb)
             sums[1] += fold(dp)
 
         def p1():
-            own = ext_ref[rows_of(m + 1), :]
+            own = own_ref[rows_of(m + 1), :]
             pds[...] = 0.5 * (mm(own, w_dst_ref[...]) + ebias_ref[...])
 
         stages = dict(
@@ -293,7 +306,7 @@
         dps[...] = jnp.concatenate(dpd, 0)
         return carry
 
-    pds[...] = 0.5 * (mm(ext_ref[pl.ds(0, chunk), :], w_dst_ref[...]) + ebias_ref[...])
+    pds[...] = 0.5 * (mm(own_ref[pl.ds(0, chunk), :], w_dst_ref[...]) + ebias_ref[...])
     lax.fori_loop(0, steps + 8, body, 0)
 
     gv_ref[...] = jnp.concatenate(
@@ -308,7 +321,7 @@
     dext = mm_nt(dpb, w_src_ref[...])
     down_ref[...] += dext[:nodes]
     halo_ref[...] = dext[nodes:].astype(BF)
-    gw_ref[0] = mm_tn(ext_ref[...], dpb)
+    gw_ref[0] = mm_tn(own_ref[...], dpb[:nodes]) + mm_tn(rim_ref[...], dpb[nodes:])
 
 
 def diagonal(w):
@@ -318,24 +331,25 @@
     )
 
 
-def layer(extended, cotangent, neighbours, node_mask, weights):
+def layer(node_latent, rims, cotangent, neighbours, node_mask, weights):
     w_src, w_dst, w_msg, edge_gain, edge_bias, w_self, w_agg, node_bias, w_out = weights
     degree, nodes = neighbours.shape
     width = cotangent.shape[1]
-    listed = extended.shape[0]
+    listed = nodes + rims.shape[0]
     chunk = min(CHUNK, nodes)
     steps = nodes // chunk
     edges = degree * chunk
     idx = jnp.where(neighbours < 0, listed, neighbours)
     idx = idx.reshape(degree, steps, chunk).transpose(0, 2, 1).reshape(-1)
-    live = jnp.broadcast_to(node_mask.astype(BF)[:, None], (nodes, width))
+    lanes = min(128, nodes)
+    mask = node_mask.reshape(nodes // lanes, lanes)
     w32 = w_msg.astype(F32)
     w_cent = (w32 - jnp.mean(w32, axis=1, keepdims=True)).astype(BF)
     half = jnp.asarray(0.5, BF)
     vmem = pl.BlockSpec(memory_space=pltpu.VMEM)
     return pl.pallas_call(
         functools.partial(layer_kernel, degree, chunk),
-        in_specs=[pl.BlockSpec(memory_space=pltpu.SMEM)] + [vmem] * 14,
+        in_specs=[pl.BlockSpec(memory_space=pltpu.SMEM)] + [vmem] * 15,
         out_specs=[vmem] * 5,
         out_shape=[
             jax.ShapeDtypeStruct((nodes, width), BF),
@@ -348,13 +362,13 @@
             pltpu.VMEM((listed + 8, width), F32),
             pltpu.VMEM((RING, edges, width), BF),
             pltpu.VMEM((RING, edges, width), F32),
-            pltpu.VMEM((RING, edges // 2, 2 * width), F32),
-            pltpu.VMEM((RING, edges // 2, 2 * width), F32),
+            pltpu.VMEM((4, edges // 2, 2 * width), F32),
+            pltpu.VMEM((4, edges // 2, 2 * width), F32),
             pltpu.VMEM((edges, width), BF),
             pltpu.VMEM((edges, width), F32),
             pltpu.VMEM((RING, chunk, width), F32),
             pltpu.VMEM((chunk, width), F32),
-            pltpu.VMEM((RING, chunk, width), F32),
+            pltpu.VMEM((5, chunk, width), F32),
             pltpu.VMEM((3, 8, width), F32),
             pltpu.VMEM((edges, width), BF),
             pltpu.VMEM((edges, width), F32),
@@ -365,6 +379,7 @@
             pltpu.VMEM((chunk, width), F32),
             pltpu.VMEM((chunk, width), BF),
             pltpu.VMEM((chunk, width), BF),
+            pltpu.VMEM((nodes, width), BF),
         ]
         + [pltpu.VMEM((listed + 24, width), F32)] * COPIES,
         compiler_params=pltpu.CompilerParams(vmem_limit_bytes=60 * 2**20),
@@ -372,8 +387,9 @@
     )(
         idx,
         cotangent,
-        live,
-        extended,
+        mask,
+        node_latent,
+        rims,
         w_src,
         w_src * half,
         w_dst,
@@ -386,6 +402,79 @@
         node_bias[None],
         w_out,
     )
+
+
+def exchange_kernel(size, list_ref, own_ref, out_ref, own32, outbound, send_sem, recv_sem):
+    rim = out_ref.shape[0] // 2
+    width = out_ref.shape[1]
+    me = lax.axis_index("tile")
+    below = lax.rem(me + size - 1, size)
+    above = lax.rem(me + 1, size)
+    barrier = pltpu.get_barrier_semaphore()
+    for other in (below, above):
+        pl.semaphore_signal(
+            barrier, inc=1, device_id={"tile": other}, device_id_type=MESH
+        )
+    own32[...] = own_ref[...].astype(F32)
+    at_row = lax.broadcasted_iota(jnp.int32, (8, width), 0)
+    bit = [(at_row & b) != 0 for b in (1, 2, 4)]
+    step = 64
+
+    def rows_at(base):
+        rows = [
+            jnp.broadcast_to(own32[pl.ds(list_ref[base + j], 1), :], (8, width))
+            for j in range(8)
+        ]
+        for b in bit:
+            rows = [jnp.where(b, q, p) for p, q in zip(rows[::2], rows[1::2])]
+        return rows[0]
+
+    def gather(t, carry):
+        base = pl.multiple_of(t * step, step)
+        part = jnp.concatenate([rows_at(base + g * 8) for g in range(step // 8)], 0)
+        outbound[pl.ds(base, step), :] = part.astype(BF)
+        return carry
+
+    def send(here, there, other, sem):
+        return pltpu.make_async_remote_copy(
+            src_ref=outbound.at[pl.ds(here, rim)],
+            dst_ref=out_ref.at[pl.ds(there, rim)],
+            send_sem=send_sem.at[sem],
+            recv_sem=recv_sem.at[sem],
+            device_id={"tile": other},
+            device_id_type=MESH,
+        )
+
+    to_above = send(rim, 0, above, 0)
+    to_below = send(0, rim, below, 1)
+    lax.fori_loop(rim // step, 2 * rim // step, gather, 0)
+    pl.semaphore_wait(barrier, 2)
+    to_above.start()
+    lax.fori_loop(0, rim // step, gather, 0)
+    to_below.start()
+    to_above.wait()
+    to_below.wait()
+
+
+def exchange(listing, node_latent, size):
+    count, width = listing.shape[0], node_latent.shape[1]
+    vmem = pl.BlockSpec(memory_space=pltpu.VMEM)
+    return pl.pallas_call(
+        functools.partial(exchange_kernel, size),
+        in_specs=[pl.BlockSpec(memory_space=pltpu.SMEM), vmem],
+        out_specs=vmem,
+        out_shape=jax.ShapeDtypeStruct((count, width), BF),
+        scratch_shapes=[
+            pltpu.VMEM(node_latent.shape, F32),
+            pltpu.VMEM((count, width), BF),
+            pltpu.SemaphoreType.DMA((2,)),
+            pltpu.SemaphoreType.DMA((2,)),
+        ],
+        compiler_params=pltpu.CompilerParams(
+            collective_id=0, has_side_effects=True, vmem_limit_bytes=32 * 2**20
+        ),
+        name="exchange",
+    )(listing, node_latent)
 
 
 def finish_kernel(list_ref, back_ref, down_ref, out_ref):
@@ -437,12 +526,9 @@
     up = [(i, (i + 1) % size) for i in range(size)]
     down = [(j, i) for i, j in up]
     listing = send_rows.reshape(1, 2 * rim)
-    outbound = node_latent[listing[0]]
-    before = lax.ppermute(outbound[rim:], "tile", up)
-    after = lax.ppermute(outbound[:rim], "tile", down)
-    extended = jnp.concatenate([node_latent, before, after], axis=0)
+    rims = exchange(listing[0], node_latent, size)
     updated, down_grad, halo, gw, gv = layer(
-        extended, cotangent, neighbours, node_mask, weights
+        node_latent, rims, cotangent, neighbours, node_mask, weights
     )
     to_below = lax.ppermute(halo[:rim], "tile", down)
     to_above = lax.ppermute(halo[rim:], "tile", up)

time: 172 us -> 170 us (0.988)
  Pallas kernels: 117 us -> 130 us
  waiting for transfers between devices: 25.3 us -> 18.2 us
  local copies, waits for them, and re-layouts: 13.8 us -> 8.05 us
  starting transfers between devices: 10.5 us -> 6.22 us
    pallas_call x0 -> x1, Pallas kernels: none -> 14.4 us  [exchange(): pl.pallas_call(functools.partial(exchange_kernel, size), in_specs=[pl.Blo...]
    ppermute x2 -> x0, waiting for transfers between devices: 8.46 us -> none  [the longest x1 8.46 us: on_device(): before = lax.ppermute(outbound[rim:], 'tile', up)]
    gather x1 -> x0, local copies, waits for them, and re-layouts: 7 us -> none  [on_device(): outbound = node_latent[listing[0]]]
    unnamed x15 -> x10, local copies, waits for them, and re-layouts: 0.97 us -> 3.84 us
    ppermute x1, starting transfers between devices: 4.36 us -> 1.54 us  [on_device(): to_above = lax.ppermute(halo[rim:], 'tile', up)]
    ppermute x3, waiting for transfers between devices: 7.11 us -> 9.86 us  [total_over(): other = lax.ppermute(value, axis, [(i, i ^ bit) for i in range(size)])]
    ppermute x2 -> x0, starting transfers between devices: 2.08 us -> none  [the longest x1 1.6 us: on_device(): before = lax.ppermute(outbound[rim:], 'tile', up)]
  transfers between devices with their start and end apart: 7 -> 5, of which waited for: 5 -> 4; matrix products, arithmetic and copies ran while one was open for 3% -> 2% of each run, Pallas kernels for 5% -> 5%
where the time goes in v2:
time: 170 us
  Pallas kernels  130 us (76%)
  waiting for transfers between devices  18.2 us (11%)
  local copies, waits for them, and re-layouts  8.05 us (5%)
  other arithmetic  6.24 us (4%)
  starting transfers between devices  6.22 us (4%)
    pallas_call x1, Pallas kernels, layer(): pl.pallas_call(functools.partial(layer_kernel, degree, chunk), in_specs=[...  107 us
    pallas_call x1, Pallas kernels, exchange(): pl.pallas_call(functools.partial(exchange_kernel, size), in_specs=[pl.Blo...  14.4 us
    ppermute x3, waiting for transfers between devices, total_over(): other = lax.ppermute(value, axis, [(i, i ^ bit) for i in range(size)])  9.86 us
    pallas_call x1, Pallas kernels, finish(): pl.pallas_call(finish_kernel, grid=(nodes // count,), in_specs=[pl.BlockS...  8.68 us
    ppermute x1, waiting for transfers between devices, on_device(): to_above = lax.ppermute(halo[rim:], 'tile', up)  4.76 us
    ppermute x3, starting transfers between devices, total_over(): other = lax.ppermute(value, axis, [(i, i ^ bit) for i in range(size)])  4.14 us
    unnamed x10, local copies, waits for them, and re-layouts  3.84 us
    ppermute x1, waiting for transfers between devices, on_device(): to_below = lax.ppermute(halo[:rim], 'tile', down)  3.61 us
  transfers between devices with their start and end apart: 5, of which 4 were waited for; matrix products, arithmetic and copies ran while one was open for 2% of the time, Pallas kernels for 5%

profile of v2, /device:TPU:14, one launch (start us, length us, event | category | flops | bytes accessed | tf_op | source)
XLA Modules:
  0.0 169.5 jit_solution(13461208501677270401)
XLA Ops:
  0.7 0.9 convert_reduce_fusion
  1.6 0.9 copy.30
  2.5 0.7 copy.35
  3.2 0.8 fusion.6
  4.0 0.9 copy.29
  4.9 0.7 copy.31.w_half_ref
  5.7 1.0 compare_select_fusion
  6.9 0.9 copy.28
  7.8 0.7 fusion.4
  8.5 14.4 %exchange.1.rim_ref = bf16[2048,128]{1,0:T(8,128)(2,1)S(1)} custom-call(s32[2048]{0:T(1024)S(1)} %bitcast.21, bf16[4096,128]{1,0:T(8,128)(2,1)S(1)} %copy-done), custom_call_target="tpu_custom_call" | custom-call | tf_op jit(solution)/shard_map/exchange/pallas_call | solution.py:462
  22.9 0.8 copy-done.1
  23.7 107.0 %layer.1 = (bf16[4096,128]{1,0:T(8,128)(2,1)}, f32[4096,128]{1,0:T(8,128)}, bf16[2048,128]{1,0:T(8,128)(2,1)}, f32[6,128,128]{2,1,0:T(8,128)}, f32[8,128]{1,0:T(8,128)}) custom-call(s32[49152]{0:T(1024)} %bitcast.25, f32[4096,128]{1,0:T(8,128)} %ct_ref.1, s32[32,128]{1,0:T(8,128)} %bitcast.29, bf16[4096,128]{1,0:T(8,128)(2,1)} %own_ref.3, ...), custom_call_target="tpu_custom_call" | custom-call | tf_op jit(solution)/shard_map/layer/pallas_call | solution.py:350
  131.4 1.0 convert.7
  132.4 1.3 collective-permute-start.2
  133.7 5.4 %collective-permute-done.2 = bf16[776,128]{1,0:T(8,128)(2,1)S(1)} collective-permute-done((bf16[776,128]{1,0:T(8,128)(2,1)S(1)}, bf16[776,128]{1,0:T(8,128)(2,1)S(1)}, u32[]{:S(2)}, u32[]{:S(2)}) %collective-permute-start.2) | collective-permute-done | bytes 198688 | tf_op jit(solution)/shard_map/ppermute | solution.py:516
  139.2 2.7 %collective-permute-start.3 = (bf16[776,128]{1,0:T(8,128)(2,1)S(1)}, bf16[776,128]{1,0:T(8,128)(2,1)S(1)}, u32[]{:S(2)}, u32[]{:S(2)}) collective-permute-start(bf16[776,128]{1,0:T(8,128)(2,1)S(1)} %add_convert_fusion.2), channel_id=1, source_target_pairs={{0,2},{1,3},{2,0},{3,1},{4,6},{5,7},{6,4},{7,5},{8,10},{9,11},{10,... | collective-permute-start | bytes 595976 | tf_op jit(solution)/shard_map/ppermute | solution.py:516
  141.9 1.1 fusion.7
  143.0 1.5 collective-permute-start
  145.7 4.5 %collective-permute-done.3 = bf16[776,128]{1,0:T(8,128)(2,1)S(1)} collective-permute-done((bf16[776,128]{1,0:T(8,128)(2,1)S(1)}, bf16[776,128]{1,0:T(8,128)(2,1)S(1)}, u32[]{:S(2)}, u32[]{:S(2)}) %collective-permute-start.3) | collective-permute-done | bytes 198688 | tf_op jit(solution)/shard_map/ppermute | solution.py:516
  150.3 4.8 %collective-permute-done = bf16[1024,128]{1,0:T(8,128)(2,1)S(1)} collective-permute-done((bf16[1024,128]{1,0:T(8,128)(2,1)S(1)}, bf16[1024,128]{1,0:T(8,128)(2,1)S(1)}, u32[]{:S(2)}, u32[]{:S(2)}) %collective-permute-start) | collective-permute-done | bytes 262176 | tf_op jit(solution)/shard_map/ppermute | solution.py:534
  155.1 3.6 %collective-permute-done.1 = bf16[1024,128]{1,0:T(8,128)(2,1)S(1)} collective-permute-done((bf16[1024,128]{1,0:T(8,128)(2,1)S(1)}, bf16[1024,128]{1,0:T(8,128)(2,1)S(1)}, u32[]{:S(2)}, u32[]{:S(2)}) %collective-permute-start.1) | collective-permute-done | bytes 262176 | tf_op jit(solution)/shard_map/ppermute | solution.py:533
  158.7 0.8 pad_maximum_fusion.back_ref
  159.5 8.7 %finish.1 = f32[4096,128]{1,0:T(8,128)} custom-call(s32[1,2048]{1,0:T(1,128)} %bitcast.26, bf16[2048,128]{1,0:T(8,128)(2,1)} %pad_maximum_fusion.back_ref, f32[4096,128]{1,0:T(8,128)} %get-tuple-element.18.down_ref), custom_call_target="tpu_custom_call" | custom-call | tf_op jit(solution)/shard_map/finish/pallas_call | solution.py:493
  168.8 0.7 fusion.8
  (19 shorter events, 2.9 us)
Async XLA Ops:
  0.6 7.9 %copy-start = (bf16[4096,128]{1,0:T(8,128)(2,1)S(1)}, bf16[4096,128]{1,0:T(8,128)(2,1)}, u32[]{:S(2)}) copy-start(bf16[4096,128]{1,0:T(8,128)(2,1)} %own_ref.3) | copy-start | bytes 3145732
  22.9 0.8 copy-start.1
  130.7 14.4 %copy-start.2 = (s32[1,2,1024]{2,1,0:T(2,128)S(1)}, s32[1,2,1024]{2,1,0:T(2,128)}, u32[]{:S(2)}) copy-start(s32[1,2,1024]{2,1,0:T(2,128)} %param.17) | copy-start | bytes 24580
  132.4 6.7 %collective-permute-start.2 = (bf16[776,128]{1,0:T(8,128)(2,1)S(1)}, bf16[776,128]{1,0:T(8,128)(2,1)S(1)}, u32[]{:S(2)}, u32[]{:S(2)}) collective-permute-start(bf16[776,128]{1,0:T(8,128)(2,1)S(1)} %pad_maximum_fusion.1), channel_id=1, source_target_pairs={{0,1},{1,0},{2,3},{3,2},{4,5},{5,4},{6,7},{7,6},{8,9},{9,8},{10,11... | collective-permute-start | bytes 595976 | tf_op jit(solution)/shard_map/ppermute | solution.py:516
  139.2 11.0 %collective-permute-start.3 = (bf16[776,128]{1,0:T(8,128)(2,1)S(1)}, bf16[776,128]{1,0:T(8,128)(2,1)S(1)}, u32[]{:S(2)}, u32[]{:S(2)}) collective-permute-start(bf16[776,128]{1,0:T(8,128)(2,1)S(1)} %add_convert_fusion.2), channel_id=1, source_target_pairs={{0,2},{1,3},{2,0},{3,1},{4,6},{5,7},{6,4},{7,5},{8,10},{9,11},{10,... | collective-permute-start | bytes 595976 | tf_op jit(solution)/shard_map/ppermute | solution.py:516
  143.0 12.1 %collective-permute-start = (bf16[1024,128]{1,0:T(8,128)(2,1)S(1)}, bf16[1024,128]{1,0:T(8,128)(2,1)S(1)}, u32[]{:S(2)}, u32[]{:S(2)}) collective-permute-start(bf16[1024,128]{1,0:T(8,128)(2,1)S(1)} %get-tuple-element.21), channel_id=1, source_target_pairs={{0,1},{1,2},{2,3},{3,4},{4,5},{5,6},{6,7},{7,0},{8,9},{9,10},{10,1... | collective-permute-start | bytes 786440 | tf_op jit(solution)/shard_map/ppermute | solution.py:534
  144.5 14.1 %collective-permute-start.1 = (bf16[1024,128]{1,0:T(8,128)(2,1)S(1)}, bf16[1024,128]{1,0:T(8,128)(2,1)S(1)}, u32[]{:S(2)}, u32[]{:S(2)}) collective-permute-start(bf16[1024,128]{1,0:T(8,128)(2,1)S(1)} %get-tuple-element.22), channel_id=1, source_target_pairs={{1,0},{2,1},{3,2},{4,3},{5,4},{6,5},{7,6},{0,7},{9,8},{10,9},{11,1... | collective-permute-start | bytes 786440 | tf_op jit(solution)/shard_map/ppermute | solution.py:533
  150.2 18.0 %collective-permute-start.4 = (bf16[776,128]{1,0:T(8,128)(2,1)S(1)}, bf16[776,128]{1,0:T(8,128)(2,1)S(1)}, u32[]{:S(2)}, u32[]{:S(2)}) collective-permute-start(bf16[776,128]{1,0:T(8,128)(2,1)S(1)} %add_convert_fusion.1), channel_id=1, source_target_pairs={{0,4},{1,5},{2,6},{3,7},{4,0},{5,1},{6,2},{7,3},{8,12},{9,13},{10,... | collective-permute-start | bytes 595976 | tf_op jit(solution)/shard_map/ppermute | solution.py:516

commit v3 on v2

--- a/solution.py
+++ b/solution.py
@@ -9,6 +9,7 @@
 
 CHUNK = 32
 RING = 8
+HALVES = 2
 COPIES = 8
 EMPTY = -1e4
 PLAN = (
@@ -44,10 +45,8 @@
     own_ref,
     rim_ref,
     w_src_ref,
-    w_half_ref,
     w_dst_ref,
-    w_back_ref,
-    w_cent_ref,
+    w_msg_ref,
     gain_ref,
     ebias_ref,
     w_self_ref,
@@ -80,6 +79,8 @@
     sbs,
     dobs,
     live_ref,
+    w_cent_ref,
+    w_back_ref,
     *accs,
 ):
     nodes, width = down_ref.shape
@@ -90,9 +91,17 @@
     half = edges // 2
     groups = edges // 8
 
-    table[pl.ds(0, nodes), :] = mm(own_ref[...], w_half_ref[...])
-    table[pl.ds(nodes, listed - nodes), :] = mm(rim_ref[...], w_half_ref[...])
-    table[pl.ds(listed, 8), :] = jnp.full((8, width), EMPTY, F32)
+    w_half = (0.5 * w_src_ref[...].astype(F32)).astype(BF)
+    table[pl.ds(8, nodes), :] = mm(own_ref[...], w_half)
+    table[pl.ds(8 + nodes, listed - nodes), :] = mm(rim_ref[...], w_half)
+    table[pl.ds(0, 8), :] = jnp.full((8, width), EMPTY, F32)
+    w32 = w_msg_ref[...].astype(F32)
+    cent = (w32 - jnp.mean(w32, axis=1, keepdims=True)).astype(BF)
+    back = (0.5 * w32).T.astype(BF)
+    for ref, w in ((w_cent_ref, cent), (w_back_ref, back)):
+        ref[...] = jnp.zeros_like(ref)
+        ref[pl.ds(0, width), pl.ds(0, width)] = w
+        ref[pl.ds(width, width), pl.ds(width, width)] = w
     for ref in (
         slope, yhat, rstd, dmsg, dhid, ysums, dycs, sums, hid, hid_new, slope_new, dps,
         cents, pres, dinners, sbs, dobs, *accs,
@@ -122,8 +131,14 @@
         return pl.ds(pl.multiple_of(jnp.clip(m, 0, steps - 1) * chunk, chunk), chunk)
 
     def list_of(m):
-        at = jnp.clip(m, 0, steps - 1)
-        return lambda e: idx_ref.at[pl.ds(e * steps, steps)][at]
+        at = jnp.clip(m, 0, steps - 1) * chunk
+        far = nodes - chunk + 1
+
+        def one(e):
+            start = e // chunk * nodes + e % chunk
+            return idx_ref.at[pl.ds(start, far)][at]
+
+        return one
 
     def body(m, carry):
         gain = gain_ref[...]
@@ -146,7 +161,7 @@
 
         def gather(g):
             rows = [
-                jnp.broadcast_to(table[pl.ds(idx0(g * 8 + j), 1), :], (8, width))
+                jnp.broadcast_to(table[pl.ds(idx0(g * 8 + j) + 8, 1), :], (8, width))
                 for j in range(8)
             ]
             for b in bit:
@@ -324,32 +339,19 @@
     gw_ref[0] = mm_tn(own_ref[...], dpb[:nodes]) + mm_tn(rim_ref[...], dpb[nodes:])
 
 
-def diagonal(w):
-    zero = jnp.zeros_like(w)
-    return jnp.concatenate(
-        [jnp.concatenate([w, zero], 1), jnp.concatenate([zero, w], 1)], 0
-    )
-
-
 def layer(node_latent, rims, cotangent, neighbours, node_mask, weights):
     w_src, w_dst, w_msg, edge_gain, edge_bias, w_self, w_agg, node_bias, w_out = weights
     degree, nodes = neighbours.shape
     width = cotangent.shape[1]
     listed = nodes + rims.shape[0]
     chunk = min(CHUNK, nodes)
-    steps = nodes // chunk
     edges = degree * chunk
-    idx = jnp.where(neighbours < 0, listed, neighbours)
-    idx = idx.reshape(degree, steps, chunk).transpose(0, 2, 1).reshape(-1)
     lanes = min(128, nodes)
     mask = node_mask.reshape(nodes // lanes, lanes)
-    w32 = w_msg.astype(F32)
-    w_cent = (w32 - jnp.mean(w32, axis=1, keepdims=True)).astype(BF)
-    half = jnp.asarray(0.5, BF)
     vmem = pl.BlockSpec(memory_space=pltpu.VMEM)
     return pl.pallas_call(
         functools.partial(layer_kernel, degree, chunk),
-        in_specs=[pl.BlockSpec(memory_space=pltpu.SMEM)] + [vmem] * 15,
+        in_specs=[pl.BlockSpec(memory_space=pltpu.SMEM)] + [vmem] * 13,
         out_specs=[vmem] * 5,
         out_shape=[
             jax.ShapeDtypeStruct((nodes, width), BF),
@@ -380,21 +382,21 @@
             pltpu.VMEM((chunk, width), BF),
             pltpu.VMEM((chunk, width), BF),
             pltpu.VMEM((nodes, width), BF),
+            pltpu.VMEM((2 * width, 2 * width), BF),
+            pltpu.VMEM((2 * width, 2 * width), BF),
         ]
         + [pltpu.VMEM((listed + 24, width), F32)] * COPIES,
         compiler_params=pltpu.CompilerParams(vmem_limit_bytes=60 * 2**20),
         name="layer",
     )(
-        idx,
+        neighbours.reshape(-1),
         cotangent,
         mask,
         node_latent,
         rims,
         w_src,
-        w_src * half,
         w_dst,
-        diagonal(w_msg.T * half),
-        diagonal(w_cent),
+        w_msg,
         edge_gain[None],
         edge_bias[None],
         w_self,
@@ -477,66 +479,169 @@
     )(listing, node_latent)
 
 
-def finish_kernel(list_ref, back_ref, down_ref, out_ref):
-    count = out_ref.shape[0]
-    first = pl.program_id(0) * count
-    span = list_ref.shape[1]
-    here = lax.broadcasted_iota(jnp.int32, (count, span), 0) + first
-    hit = jnp.where(here == list_ref[...], 1.0, 0.0).astype(BF)
-    out_ref[...] = down_ref[...] + mm(hit, back_ref[...])
-
-
-def finish(listing, back, down):
+def finish_kernel(
+    size,
+    scale,
+    list_ref,
+    halo_ref,
+    down_ref,
+    gw_ref,
+    gv_ref,
+    out_ref,
+    total_ref,
+    back,
+    packed,
+    parts,
+    mine,
+    gathered,
+    halo_send,
+    halo_recv,
+    part_send,
+    part_recv,
+    full_send,
+    full_recv,
+):
+    nodes, width = out_ref.shape
+    rim = halo_ref.shape[0] // 2
+    piece = mine.shape[0]
+    me = lax.axis_index("tile")
+    others = [lax.rem(me + d, size) for d in range(1, size)]
+    barrier = pltpu.get_barrier_semaphore()
+    for other in others:
+        pl.semaphore_signal(
+            barrier, inc=1, device_id={"tile": other}, device_id_type=MESH
+        )
+
+    def copy(src, dst, send, recv, other):
+        return pltpu.make_async_remote_copy(
+            src_ref=src,
+            dst_ref=dst,
+            send_sem=send,
+            recv_sem=recv,
+            device_id={"tile": other},
+            device_id_type=MESH,
+        )
+
+    mats = gw_ref.shape[0] * width
+    for i in range(gw_ref.shape[0]):
+        packed[pl.ds(i * width, width), :] = gw_ref[i].astype(BF)
+    rest = packed.shape[0] - mats
+    packed[pl.ds(mats, rest), :] = jnp.concatenate(
+        [gv_ref[...], jnp.zeros((rest - gv_ref.shape[0], width), F32)], 0
+    ).astype(BF)
+
+    def piece_of(ref, at):
+        return ref.at[pl.ds(pl.multiple_of(at * piece, 16), piece)]
+
+    spread = [
+        copy(piece_of(packed, o), parts.at[d], part_send.at[d], part_recv.at[d], o)
+        for d, o in enumerate(others)
+    ]
+    share = [
+        copy(mine, piece_of(gathered, me), full_send.at[d], full_recv.at[d], o)
+        for d, o in enumerate(others)
+    ]
+    span = rim // HALVES
+    homes = []
+    for i in range(HALVES):
+        for here, there, other in ((rim, 0, others[0]), (0, rim, others[-1])):
+            n = len(homes)
+            homes.append(
+                (
+                    there + i * span,
+                    copy(
+                        halo_ref.at[pl.ds(here + i * span, span)],
+                        back.at[pl.ds(there + i * span, span)],
+                        halo_send.at[n],
+                        halo_recv.at[n],
+                        other,
+                    ),
+                )
+            )
+
+    pl.semaphore_wait(barrier, size - 1)
+    for c in spread:
+        c.start()
+    for _, c in homes[:2]:
+        c.start()
+    out_ref[...] = down_ref[...]
+    for c in spread:
+        c.wait_recv()
+    total = packed[pl.ds(pl.multiple_of(me * piece, 16), piece), :].astype(F32)
+    for d in range(size - 1):
+        total = total + parts[d].astype(F32)
+    mine[...] = total.astype(BF)
+    gathered[pl.ds(pl.multiple_of(me * piece, 16), piece), :] = total.astype(BF)
+    for c in share:
+        c.start()
+    for _, c in homes[2:]:
+        c.start()
+
+    rows = min(512, nodes)
+    for at, c in homes:
+        c.wait_recv()
+
+        def place(b, carry):
+            first = pl.multiple_of(b * rows, rows)
+            here = lax.broadcasted_iota(jnp.int32, (rows, span), 0) + first
+            hit = jnp.where(here == list_ref[:, at : at + span], 1.0, 0.0).astype(BF)
+            out_ref[pl.ds(first, rows), :] += mm(hit, back[pl.ds(at, span), :])
+            return carry
+
+        lax.fori_loop(0, nodes // rows, place, 0)
+
+    for c in share:
+        c.wait_recv()
+    total_ref[...] = gathered[...].astype(F32) * scale
+    for c in spread + share + [c for _, c in homes]:
+        c.wait_send()
+
+
+def finish(listing, halo, down, gw, gv, size, scale):
     nodes, width = down.shape
-    count = min(512, nodes)
-    rowed = pl.BlockSpec((count, width), lambda i: (i, 0))
+    need = gw.shape[0] * gw.shape[1] + gv.shape[0]
+    piece = -(-need // (16 * size)) * 16
+    vmem = pl.BlockSpec(memory_space=pltpu.VMEM)
+    dma = pltpu.SemaphoreType.DMA
     return pl.pallas_call(
-        finish_kernel,
-        grid=(nodes // count,),
-        in_specs=[
-            pl.BlockSpec((1, listing.shape[1]), lambda i: (0, 0)),
-            pl.BlockSpec(back.shape, lambda i: (0, 0)),
-            rowed,
+        functools.partial(finish_kernel, size, scale),
+        in_specs=[vmem] * 5,
+        out_specs=[vmem] * 2,
+        out_shape=[
+            jax.ShapeDtypeStruct((nodes, width), F32),
+            jax.ShapeDtypeStruct((size * piece, width), F32),
         ],
-        out_specs=rowed,
-        out_shape=jax.ShapeDtypeStruct((nodes, width), F32),
+        scratch_shapes=[
+            pltpu.VMEM(halo.shape, BF),
+            pltpu.VMEM((size * piece, width), BF),
+            pltpu.VMEM((size - 1, piece, width), BF),
+            pltpu.VMEM((piece, width), BF),
+            pltpu.VMEM((size * piece, width), BF),
+            dma((2 * HALVES,)),
+            dma((2 * HALVES,)),
+            dma((size - 1,)),
+            dma((size - 1,)),
+            dma((size - 1,)),
+            dma((size - 1,)),
+        ],
         compiler_params=pltpu.CompilerParams(
-            dimension_semantics=("arbitrary",), vmem_limit_bytes=60 * 2**20
+            collective_id=1, has_side_effects=True, vmem_limit_bytes=32 * 2**20
         ),
         name="finish",
-    )(listing, back, down)
-
-
-def total_over(value, axis):
-    size = lax.axis_size(axis)
-    if size & (size - 1):
-        return lax.psum(value, axis)
-    bit = 1
-    while bit < size:
-        other = lax.ppermute(value, axis, [(i, i ^ bit) for i in range(size)])
-        value = (value.astype(F32) + other.astype(F32)).astype(BF)
-        bit *= 2
-    return value
+    )(listing, halo, down, gw, gv)
 
 
 def on_device(node_latent, cotangent, neighbours, send_rows, node_mask, *weights):
     nodes = node_latent.shape[0]
-    rim = send_rows.shape[2]
     size = lax.axis_size("tile")
-    up = [(i, (i + 1) % size) for i in range(size)]
-    down = [(j, i) for i, j in up]
-    listing = send_rows.reshape(1, 2 * rim)
+    listing = send_rows.reshape(1, -1)
     rims = exchange(listing[0], node_latent, size)
     updated, down_grad, halo, gw, gv = layer(
         node_latent, rims, cotangent, neighbours, node_mask, weights
     )
-    to_below = lax.ppermute(halo[:rim], "tile", down)
-    to_above = lax.ppermute(halo[rim:], "tile", up)
-    back = jnp.concatenate([to_above, to_below], axis=0)
-    packed = jnp.concatenate([gw.reshape(-1, gw.shape[2]), gv], axis=0).astype(BF)
-    packed = total_over(packed, "tile").astype(F32)
-    latent_grad = finish(listing, back, down_grad)
-    packed = packed * (nodes * size) ** (-0.5)
+    latent_grad, packed = finish(
+        listing, halo, down_grad, gw, gv, size, (nodes * size) ** (-0.5)
+    )
     width = gw.shape[2]
     mats = [packed[i * width : (i + 1) * width] for i in range(6)]
     vecs = [packed[6 * width + i] for i in range(3)]

time: 170 us -> 162 us (0.953); the launches traced: 170 us -> 159 us
  waiting for transfers between devices: 18.2 us -> 0 us
  Pallas kernels: 130 us -> 147 us
  other arithmetic: 6.24 us -> 0 us
  starting transfers between devices: 6.22 us -> 0 us
  local copies, waits for them, and re-layouts: 8.05 us -> 12 us
    ppermute x5 -> x0, waiting for transfers between devices: 18.2 us -> none  [the longest x3 9.86 us: total_over(): other = lax.ppermute(value, axis, [(i, i ^ bit) for i in range(size)])]
    pallas_call x1, Pallas kernels: 8.68 us -> 26.7 us  [finish(): pl.pallas_call(functools.partial(finish_kernel, size, scale), in_specs=[v...]
    ppermute x5 -> x0, starting transfers between devices: 6.22 us -> none  [the longest x3 4.14 us: total_over(): other = lax.ppermute(value, axis, [(i, i ^ bit) for i in range(size)])]
    unnamed x10 -> x15, local copies, waits for them, and re-layouts: 3.84 us -> 9.05 us
    another operation x2 -> x0, other arithmetic: 1.72 us -> none
  transfers between devices with their start and end apart: 5 -> 0, of which waited for: 4 -> 0; matrix products, arithmetic and copies ran while one was open for 2% -> 0% of each run, Pallas kernels for 5% -> 0%
where the time goes in v3:
time: 162 us; the launch traced here: 159 us
  Pallas kernels  147 us (91%)
  local copies, waits for them, and re-layouts  12 us (7%)
    pallas_call x1, Pallas kernels, layer(): pl.pallas_call(functools.partial(layer_kernel, degree, chunk), in_specs=[...  106 us
    pallas_call x1, Pallas kernels, finish(): pl.pallas_call(functools.partial(finish_kernel, size, scale), in_specs=[v...  26.7 us
    pallas_call x1, Pallas kernels, exchange(): pl.pallas_call(functools.partial(exchange_kernel, size), in_specs=[pl.Blo...  14.4 us
    unnamed x15, local copies, waits for them, and re-layouts  9.05 us

profile of v3, /device:TPU:14, one launch (start us, length us, event | category | flops | bytes accessed | tf_op | source)
XLA Modules:
  0.0 159.5 jit_solution(17736522694170699987)
XLA Ops:
  0.6 0.7 copy.28
  1.3 0.7 copy.26
  2.1 1.7 %reshape.31.idx_ref = s32[49152]{0:T(1024)} reshape(s32[12,4096]{1,0:T(8,128)} %param.16) | data formatting | bytes 393216 | tf_op jit(solution)/shard_map/reshape | solution.py:392
  3.7 0.0 copy-start
  3.7 1.2 copy-done
  5.0 14.4 %exchange.1.rim_ref = bf16[2048,128]{1,0:T(8,128)(2,1)S(1)} custom-call(s32[2048]{0:T(1024)S(1)} %bitcast.17, bf16[4096,128]{1,0:T(8,128)(2,1)S(1)} %copy-done), custom_call_target="tpu_custom_call" | custom-call | tf_op jit(solution)/shard_map/exchange/pallas_call | solution.py:464
  19.4 0.0 copy-start.1
  19.4 0.8 copy-done.1
  20.2 105.8 %layer.1 = (bf16[4096,128]{1,0:T(8,128)(2,1)}, f32[4096,128]{1,0:T(8,128)}, bf16[2048,128]{1,0:T(8,128)(2,1)}, f32[6,128,128]{2,1,0:T(8,128)}, f32[8,128]{1,0:T(8,128)}) custom-call(s32[49152]{0:T(1024)} %reshape.31.idx_ref, f32[4096,128]{1,0:T(8,128)} %ct_ref.1, s32[32,128]{1,0:T(8,128)} %bitcast.20, bf16[4096,128]{1,0:T(8,128)(2,1)} %own_ref.3, ...), custom_call_target="tpu_custom_call" | custom-call | tf_op jit(solution)/shard_map/layer/pallas_call | solution.py:352
  125.9 0.0 copy-start.2
  125.9 1.6 copy-done.2
  127.5 0.0 copy-start.3
  127.5 1.0 copy-done.3
  128.5 0.0 copy-start.4
  128.5 1.0 copy-done.4
  129.5 0.0 copy-start.5
  129.5 0.7 copy-done.5
  130.2 26.7 %finish.1 = (f32[4096,128]{1,0:T(8,128)S(1)}, f32[896,128]{1,0:T(8,128)S(1)}) custom-call(s32[1,2048]{1,0:T(1,128)S(1)} %bitcast.16, bf16[2048,128]{1,0:T(8,128)(2,1)S(1)} %copy-done.3, f32[4096,128]{1,0:T(8,128)S(1)} %copy-done.2, f32[6,128,128]{2,1,0:T(8,128)S(1)} %copy-done.4, f32[8,128]{1,0:T(8,128)S(1)} %copy-done.5), custom_call_target="tpu_custom_call" | custom-call | tf_op jit(solution)/shard_map/finish/pallas_call | solution.py:606
  156.9 0.5 slice_bitcast_fusion
  157.4 0.7 fusion
  158.2 1.3 copy.30
Async XLA Ops:
  3.7 1.2 copy-start
  19.4 0.8 copy-start.1
  125.9 1.6 copy-start.2
  127.5 1.0 copy-start.3
  128.5 1.0 copy-start.4
  129.5 0.7 copy-start.5

commit v4 on v3

--- a/solution.py
+++ b/solution.py
@@ -39,8 +39,8 @@
 def layer_kernel(
     degree,
     chunk,
-    idx_ref,
-    ct_ref,
+    idx_hbm,
+    ct_hbm,
     mask_ref,
     own_ref,
     rim_ref,
@@ -53,11 +53,10 @@
     w_agg_ref,
     nbias_ref,
     w_out_ref,
-    updated_ref,
+    updated_hbm,
     down_ref,
     halo_ref,
-    gw_ref,
-    gv_ref,
+    packed_ref,
     table,
     hid,
     slope,
@@ -81,8 +80,17 @@
     live_ref,
     w_cent_ref,
     w_back_ref,
+    gw_ref,
+    idx_ref,
+    ct_ref,
+    updated_ref,
+    local_sem,
     *accs,
 ):
+    fetch_idx = pltpu.make_async_copy(idx_hbm, idx_ref, local_sem.at[0])
+    fetch_ct = pltpu.make_async_copy(ct_hbm, ct_ref, local_sem.at[1])
+    fetch_idx.start()
+    fetch_ct.start()
     nodes, width = down_ref.shape
     listed = nodes + rim_ref.shape[0]
     copies = len(accs)
@@ -322,13 +330,12 @@
         return carry
 
     pds[...] = 0.5 * (mm(own_ref[pl.ds(0, chunk), :], w_dst_ref[...]) + ebias_ref[...])
+    fetch_idx.wait()
+    fetch_ct.wait()
     lax.fori_loop(0, steps + 8, body, 0)
-
-    gv_ref[...] = jnp.concatenate(
-        [jnp.sum(sums[i], axis=0, keepdims=True) for i in range(3)]
-        + [jnp.zeros((5, width), F32)],
-        0,
-    )
+    put_updated = pltpu.make_async_copy(updated_ref, updated_hbm, local_sem.at[2])
+    put_updated.start()
+
     dproj = accs[0][pl.ds(8, listed), :]
     for acc in accs[1:]:
         dproj = dproj + acc[pl.ds(8, listed), :]
@@ -337,9 +344,18 @@
     down_ref[...] += dext[:nodes]
     halo_ref[...] = dext[nodes:].astype(BF)
     gw_ref[0] = mm_tn(own_ref[...], dpb[:nodes]) + mm_tn(rim_ref[...], dpb[nodes:])
-
-
-def layer(node_latent, rims, cotangent, neighbours, node_mask, weights):
+    for i in range(gw_ref.shape[0]):
+        packed_ref[pl.ds(i * width, width), :] = gw_ref[i].astype(BF)
+    mats = gw_ref.shape[0] * width
+    packed_ref[pl.ds(mats, packed_ref.shape[0] - mats), :] = jnp.concatenate(
+        [jnp.sum(sums[i], axis=0, keepdims=True) for i in range(3)]
+        + [jnp.zeros((packed_ref.shape[0] - mats - 3, width), F32)],
+        0,
+    ).astype(BF)
+    put_updated.wait()
+
+
+def layer(node_latent, rims, cotangent, neighbours, node_mask, weights, packed):
     w_src, w_dst, w_msg, edge_gain, edge_bias, w_self, w_agg, node_bias, w_out = weights
     degree, nodes = neighbours.shape
     width = cotangent.shape[1]
@@ -349,16 +365,16 @@
     lanes = min(128, nodes)
     mask = node_mask.reshape(nodes // lanes, lanes)
     vmem = pl.BlockSpec(memory_space=pltpu.VMEM)
+    hbm = pl.BlockSpec(memory_space=pl.ANY)
     return pl.pallas_call(
         functools.partial(layer_kernel, degree, chunk),
-        in_specs=[pl.BlockSpec(memory_space=pltpu.SMEM)] + [vmem] * 13,
-        out_specs=[vmem] * 5,
+        in_specs=[hbm, hbm] + [vmem] * 12,
+        out_specs=[hbm] + [vmem] * 3,
         out_shape=[
             jax.ShapeDtypeStruct((nodes, width), BF),
             jax.ShapeDtypeStruct((nodes, width), F32),
             jax.ShapeDtypeStruct((listed - nodes, width), BF),
-            jax.ShapeDtypeStruct((6, width, width), F32),
-            jax.ShapeDtypeStruct((8, width), F32),
+            jax.ShapeDtypeStruct((packed, width), BF),
         ],
         scratch_shapes=[
             pltpu.VMEM((listed + 8, width), F32),
@@ -384,6 +400,11 @@
             pltpu.VMEM((nodes, width), BF),
             pltpu.VMEM((2 * width, 2 * width), BF),
             pltpu.VMEM((2 * width, 2 * width), BF),
+            pltpu.VMEM((6, width, width), F32),
+            pltpu.SMEM((degree * nodes,), jnp.int32),
+            pltpu.VMEM((nodes, width), F32),
+            pltpu.VMEM((nodes, width), BF),
+            pltpu.SemaphoreType.DMA((3,)),
         ]
         + [pltpu.VMEM((listed + 24, width), F32)] * COPIES,
         compiler_params=pltpu.CompilerParams(vmem_limit_bytes=60 * 2**20),
@@ -406,7 +427,11 @@
     )
 
 
-def exchange_kernel(size, list_ref, own_ref, out_ref, own32, outbound, send_sem, recv_sem):
+def exchange_kernel(
+    size, list_ref, own_ref, out_ref, own16, own32, outbound, send_sem, recv_sem, local_sem
+):
+    fetch = pltpu.make_async_copy(own_ref, own16, local_sem)
+    fetch.start()
     rim = out_ref.shape[0] // 2
     width = out_ref.shape[1]
     me = lax.axis_index("tile")
@@ -417,7 +442,8 @@
         pl.semaphore_signal(
             barrier, inc=1, device_id={"tile": other}, device_id_type=MESH
         )
-    own32[...] = own_ref[...].astype(F32)
+    fetch.wait()
+    own32[...] = own16[...].astype(F32)
     at_row = lax.broadcasted_iota(jnp.int32, (8, width), 0)
     bit = [(at_row & b) != 0 for b in (1, 2, 4)]
     step = 64
@@ -437,25 +463,27 @@
         outbound[pl.ds(base, step), :] = part.astype(BF)
         return carry
 
-    def send(here, there, other, sem):
-        return pltpu.make_async_remote_copy(
-            src_ref=outbound.at[pl.ds(here, rim)],
-            dst_ref=out_ref.at[pl.ds(there, rim)],
-            send_sem=send_sem.at[sem],
-            recv_sem=recv_sem.at[sem],
-            device_id={"tile": other},
-            device_id_type=MESH,
-        )
-
-    to_above = send(rim, 0, above, 0)
-    to_below = send(0, rim, below, 1)
-    lax.fori_loop(rim // step, 2 * rim // step, gather, 0)
-    pl.semaphore_wait(barrier, 2)
-    to_above.start()
-    lax.fori_loop(0, rim // step, gather, 0)
-    to_below.start()
-    to_above.wait()
-    to_below.wait()
+    span = rim // HALVES
+    sent = []
+    for i in range(HALVES):
+        for here, there, other in ((rim, 0, above), (0, rim, below)):
+            n = len(sent)
+            start = here + i * span
+            lax.fori_loop(start // step, (start + span) // step, gather, 0)
+            if n == 0:
+                pl.semaphore_wait(barrier, 2)
+            c = pltpu.make_async_remote_copy(
+                src_ref=outbound.at[pl.ds(start, span)],
+                dst_ref=out_ref.at[pl.ds(there + i * span, span)],
+                send_sem=send_sem.at[n],
+                recv_sem=recv_sem.at[n],
+                device_id={"tile": other},
+                device_id_type=MESH,
+            )
+            c.start()
+            sent.append(c)
+    for c in sent:
+        c.wait()
 
 
 def exchange(listing, node_latent, size):
@@ -463,17 +491,22 @@
     vmem = pl.BlockSpec(memory_space=pltpu.VMEM)
     return pl.pallas_call(
         functools.partial(exchange_kernel, size),
-        in_specs=[pl.BlockSpec(memory_space=pltpu.SMEM), vmem],
+        in_specs=[
+            pl.BlockSpec(memory_space=pltpu.SMEM),
+            pl.BlockSpec(memory_space=pl.ANY),
+        ],
         out_specs=vmem,
         out_shape=jax.ShapeDtypeStruct((count, width), BF),
         scratch_shapes=[
+            pltpu.VMEM(node_latent.shape, BF),
             pltpu.VMEM(node_latent.shape, F32),
             pltpu.VMEM((count, width), BF),
-            pltpu.SemaphoreType.DMA((2,)),
-            pltpu.SemaphoreType.DMA((2,)),
+            pltpu.SemaphoreType.DMA((2 * HALVES,)),
+            pltpu.SemaphoreType.DMA((2 * HALVES,)),
+            pltpu.SemaphoreType.DMA,
         ],
         compiler_params=pltpu.CompilerParams(
-            collective_id=0, has_side_effects=True, vmem_limit_bytes=32 * 2**20
+            collective_id=0, has_side_effects=True, vmem_limit_bytes=60 * 2**20
         ),
         name="exchange",
     )(listing, node_latent)
@@ -485,12 +518,11 @@
     list_ref,
     halo_ref,
     down_ref,
-    gw_ref,
-    gv_ref,
+    packed,
     out_ref,
     total_ref,
     back,
-    packed,
+    halo,
     parts,
     mine,
     gathered,
@@ -500,9 +532,14 @@
     part_recv,
     full_send,
     full_recv,
+    local_sem,
 ):
     nodes, width = out_ref.shape
     rim = halo_ref.shape[0] // 2
+    fetch_halo = pltpu.make_async_copy(halo_ref, halo, local_sem.at[0])
+    fetch_down = pltpu.make_async_copy(down_ref, out_ref, local_sem.at[1])
+    fetch_halo.start()
+    fetch_down.start()
     piece = mine.shape[0]
     me = lax.axis_index("tile")
     others = [lax.rem(me + d, size) for d in range(1, size)]
@@ -521,14 +558,6 @@
             device_id={"tile": other},
             device_id_type=MESH,
         )
-
-    mats = gw_ref.shape[0] * width
-    for i in range(gw_ref.shape[0]):
-        packed[pl.ds(i * width, width), :] = gw_ref[i].astype(BF)
-    rest = packed.shape[0] - mats
-    packed[pl.ds(mats, rest), :] = jnp.concatenate(
-        [gv_ref[...], jnp.zeros((rest - gv_ref.shape[0], width), F32)], 0
-    ).astype(BF)
 
     def piece_of(ref, at):
         return ref.at[pl.ds(pl.multiple_of(at * piece, 16), piece)]
@@ -550,7 +579,7 @@
                 (
                     there + i * span,
                     copy(
-                        halo_ref.at[pl.ds(here + i * span, span)],
+                        halo.at[pl.ds(here + i * span, span)],
                         back.at[pl.ds(there + i * span, span)],
                         halo_send.at[n],
                         halo_recv.at[n],
@@ -562,9 +591,9 @@
     pl.semaphore_wait(barrier, size - 1)
     for c in spread:
         c.start()
+    fetch_halo.wait()
     for _, c in homes[:2]:
         c.start()
-    out_ref[...] = down_ref[...]
     for c in spread:
         c.wait_recv()
     total = packed[pl.ds(pl.multiple_of(me * piece, 16), piece), :].astype(F32)
@@ -577,6 +606,7 @@
     for _, c in homes[2:]:
         c.start()
 
+    fetch_down.wait()
     rows = min(512, nodes)
     for at, c in homes:
         c.wait_recv()
@@ -597,15 +627,15 @@
         c.wait_send()
 
 
-def finish(listing, halo, down, gw, gv, size, scale):
+def finish(listing, halo, down, packed, size, scale):
     nodes, width = down.shape
-    need = gw.shape[0] * gw.shape[1] + gv.shape[0]
-    piece = -(-need // (16 * size)) * 16
+    piece = packed.shape[0] // size
     vmem = pl.BlockSpec(memory_space=pltpu.VMEM)
+    hbm = pl.BlockSpec(memory_space=pl.ANY)
     dma = pltpu.SemaphoreType.DMA
     return pl.pallas_call(
         functools.partial(finish_kernel, size, scale),
-        in_specs=[vmem] * 5,
+        in_specs=[vmem, hbm, hbm, vmem],
         out_specs=[vmem] * 2,
         out_shape=[
             jax.ShapeDtypeStruct((nodes, width), F32),
@@ -613,7 +643,7 @@
         ],
         scratch_shapes=[
             pltpu.VMEM(halo.shape, BF),
-            pltpu.VMEM((size * piece, width), BF),
+            pltpu.VMEM(halo.shape, BF),
             pltpu.VMEM((size - 1, piece, width), BF),
             pltpu.VMEM((piece, width), BF),
             pltpu.VMEM((size * piece, width), BF),
@@ -623,12 +653,13 @@
             dma((size - 1,)),
             dma((size - 1,)),
             dma((size - 1,)),
+            dma((2,)),
         ],
         compiler_params=pltpu.CompilerParams(
-            collective_id=1, has_side_effects=True, vmem_limit_bytes=32 * 2**20
+            collective_id=1, has_side_effects=True, vmem_limit_bytes=60 * 2**20
         ),
         name="finish",
-    )(listing, halo, down, gw, gv)
+    )(listing, halo, down, packed)
 
 
 def on_device(node_latent, cotangent, neighbours, send_rows, node_mask, *weights):
@@ -636,13 +667,15 @@
     size = lax.axis_size("tile")
     listing = send_rows.reshape(1, -1)
     rims = exchange(listing[0], node_latent, size)
-    updated, down_grad, halo, gw, gv = layer(
-        node_latent, rims, cotangent, neighbours, node_mask, weights
+    width = node_latent.shape[1]
+    need = 6 * width + 3
+    piece = -(-need // (16 * size)) * 16
+    updated, down_grad, halo, packed = layer(
+        node_latent, rims, cotangent, neighbours, node_mask, weights, size * piece
     )
     latent_grad, packed = finish(
-        listing, halo, down_grad, gw, gv, size, (nodes * size) ** (-0.5)
+        listing, halo, down_grad, packed, size, (nodes * size) ** (-0.5)
     )
-    width = gw.shape[2]
     mats = [packed[i * width : (i + 1) * width] for i in range(6)]
     vecs = [packed[6 * width + i] for i in range(3)]
     return (

time: 162 us -> 163 us (level)
  Pallas kernels: 147 us -> 150 us
    unnamed x15 -> x3, local copies, waits for them, and re-layouts: 9.05 us -> 5.64 us
    pallas_call x1, Pallas kernels: 26.7 us -> 29 us  [finish(): pl.pallas_call(functools.partial(finish_kernel, size, scale), in_specs=[v...]
where the time goes in v4:
time: 163 us; the launch traced here: 161 us
  Pallas kernels  150 us (92%)
  local copies, waits for them, and re-layouts  10.4 us (6%)
    pallas_call x1, Pallas kernels, layer(): pl.pallas_call(functools.partial(layer_kernel, degree, chunk), in_specs=[...  105 us
    pallas_call x1, Pallas kernels, finish(): pl.pallas_call(functools.partial(finish_kernel, size, scale), in_specs=[v...  29 us
    pallas_call x1, Pallas kernels, exchange(): pl.pallas_call(functools.partial(exchange_kernel, size), in_specs=[pl.Blo...  15.9 us
    unnamed x3, local copies, waits for them, and re-layouts  5.64 us

profile of v4, /device:TPU:14, one launch (start us, length us, event | category | flops | bytes accessed | tf_op | source)
XLA Modules:
  0.0 161.0 jit_solution(8179679015383848482)
XLA Ops:
  0.6 1.3 copy.28
  1.9 1.3 copy.26
  3.2 1.7 %reshape.31.idx_hbm = s32[49152]{0:T(1024)} reshape(s32[12,4096]{1,0:T(8,128)} %param.16) | data formatting | bytes 393216 | tf_op jit(solution)/shard_map/reshape | solution.py:413
  4.9 15.9 %exchange.1.rim_ref = bf16[2048,128]{1,0:T(8,128)(2,1)} custom-call(s32[2048]{0:T(1024)} %bitcast.17, bf16[4096,128]{1,0:T(8,128)(2,1)} %own_ref.3), custom_call_target="tpu_custom_call" | custom-call | tf_op jit(solution)/shard_map/exchange/pallas_call | solution.py:492
  20.9 105.0 %layer.1 = (bf16[4096,128]{1,0:T(8,128)(2,1)}, f32[4096,128]{1,0:T(8,128)}, bf16[2048,128]{1,0:T(8,128)(2,1)}, bf16[896,128]{1,0:T(8,128)(2,1)}) custom-call(s32[49152]{0:T(1024)} %reshape.31.idx_hbm, f32[4096,128]{1,0:T(8,128)} %ct_hbm.1, s32[32,128]{1,0:T(8,128)} %bitcast.20, bf16[4096,128]{1,0:T(8,128)(2,1)} %own_ref.3, ...), custom_call_target="tpu_custom_call" | custom-call | tf_op jit(solution)/shard_map/layer/pallas_call | solution.py:369
  125.9 29.0 %finish.1 = (f32[4096,128]{1,0:T(8,128)}, f32[896,128]{1,0:T(8,128)}) custom-call(s32[1,2048]{1,0:T(1,128)} %bitcast.16, bf16[2048,128]{1,0:T(8,128)(2,1)} %get-tuple-element.18.halo_ref, f32[4096,128]{1,0:T(8,128)} %get-tuple-element.19.down_ref, bf16[896,128]{1,0:T(8,128)(2,1)} %get-tuple-element.20.packed), custom_call_target="tpu_custom_call" | custom-call | tf_op jit(solution)/shard_map/finish/pallas_call | solution.py:636
  154.9 1.3 slice_bitcast_fusion
  156.2 1.7 %fusion = (f32[128,128]{1,0:T(8,128)}, f32[128,128]{1,0:T(8,128)}, f32[128,128]{1,0:T(8,128)}, f32[128,128]{1,0:T(8,128)}, f32[128,128]{1,0:T(8,128)}, /*index=5*/f32[128,128]{1,0:T(8,128)}) fusion(f32[896,128]{1,0:T(8,128)} %get-tuple-element.22), kind=kLoop, calls=%fused_computation.4 | loop fusion | bytes 786432 | tf_op jit(solution)/shard_map/slice | solution.py:679
  158.0 3.0 %copy.30 = f32[4096,128]{1,0:T(8,128)} copy(f32[4096,128]{1,0:T(8,128)} %get-tuple-element.44) | data formatting | bytes 4194304
